TPU v7x, 32 devices: a whole 2x2x4 slice. The times are simulated.
32 devices in a mesh: dp: 2 (over x), seq: 4 (over z), tensor: 4 (over y, core).
Axes of the slice: x: 2, y: 2, z: 4, core: 2. Of those that a mesh axis runs over, the one named last changes fastest.
Arguments:
- block_input: bfloat16 [4096, 4, 1536], P(('seq', 'tensor'), 'dp'), may hold values from -6 to 6
- gain_in: float32 [1536], replicated, may hold values from 0.1 to 1.9
- w_zx: bfloat16 [1536, 2, 3072], P(('dp', 'seq'), None, 'tensor'), may hold values from -0.15625 to 0.15625
- w_bc: bfloat16 [1536, 2, 128], P(('dp', 'seq')), may hold values from -0.15625 to 0.15625
- w_dt: bfloat16 [1536, 48], P(('dp', 'seq'), 'tensor'), may hold values from -0.15625 to 0.15625
- conv_x: float32 [4, 3072], P(None, 'tensor'), may hold values from -3 to 3
- conv_x_b: float32 [3072], P('tensor'), may hold values from -0.5 to 0.5
- conv_bc: float32 [4, 2, 128], replicated, may hold values from -3 to 3
- conv_bc_b: float32 [2, 128], replicated, may hold values from -0.5 to 0.5
- dt_bias: float32 [48], P('tensor'), may hold values from -6.5 to -2.5
- a_log: float32 [48], P('tensor'), may hold values from 0 to 2.7
- d_skip: float32 [48], P('tensor'), may hold values from 0.5 to 1.5
- gain_norm: float32 [3072], P('tensor'), may hold values from 0.1 to 1.9
- w_out: bfloat16 [1536, 3072], P(('dp', 'seq'), 'tensor'), may hold values from -0.109375 to 0.109375
- cotangent: bfloat16 [4096, 4, 1536], P(('seq', 'tensor'), 'dp'), may hold values from -6 to 6
Outputs:
- block_output: bfloat16 [4096, 4, 1536], P(('seq', 'tensor'), 'dp')
- input_grad: bfloat16 [4096, 4, 1536], P(('seq', 'tensor'), 'dp')
- grad_gain_in: float32 [1536], replicated
- grad_w_zx: float32 [1536, 2, 3072], P(('dp', 'seq'), None, 'tensor')
- grad_w_bc: float32 [1536, 2, 128], P(('dp', 'seq'))
- grad_w_dt: float32 [1536, 48], P(('dp', 'seq'), 'tensor')
- grad_conv_x: float32 [4, 3072], P(None, 'tensor')
- grad_conv_x_b: float32 [3072], P('tensor')
- grad_conv_bc: float32 [4, 2, 128], replicated
- grad_conv_bc_b: float32 [2, 128], replicated
- grad_dt_bias: float32 [48], P('tensor')
- grad_a_log: float32 [48], P('tensor')
- grad_d_skip: float32 [48], P('tensor')
- grad_gain_norm: float32 [3072], P('tensor')
- grad_w_out: float32 [1536, 3072], P(('dp', 'seq'), 'tensor')
All inputs are finite; a program needn't handle non-finite values.
Results may differ from a plain program's by a relative error of at most 0.012.
Values may be sent and summed in bfloat16 or wider, within the bound.
A program may use at most 320 MiB of HBM per device.

v0:
```python
import jax
import jax.numpy as jnp
from jax import lax
from jax.sharding import PartitionSpec as P

L = 256
SEQ_MB = 1
MICRO = 2


epsilon = 1e-05
highest = lax.Precision.HIGHEST


def shifted(shard, axis, by):
    peers = lax.axis_size(axis)
    pairs = [(i, i + by) for i in range(peers) if 0 <= i + by < peers]
    return lax.ppermute(shard, axis, pairs)


def prefix_2(value, axis, join, neutral):
    count, mine = (lax.axis_size(axis), lax.axis_index(axis))
    pieces = jax.tree.map(lambda part: lax.all_gather(part, axis), value)
    total = jax.tree.map(
        lambda part, zero: jnp.full_like(part, 0) + jnp.asarray(zero, part.dtype), value, neutral
    )

    def prefix_lap(position, total):
        longer = join(total, jax.tree.map(lambda part: part[position], pieces))
        return jax.tree.map(lambda new, old: jnp.where(position < mine, new, old), longer, total)

    return lax.fori_loop(0, count - 1, prefix_lap, total)


def entering_2(shard, axis, combine, identity):
    peers, position = (lax.axis_size(axis), lax.axis_index(axis))
    everything = jax.tree.map(
        lambda part, kind: lax.all_gather(part.astype(kind), axis),
        shard,
        jax.tree.map(lambda a: jnp.bfloat16 if a.dtype == jnp.float32 else a.dtype, shard),
    )
    start = jax.tree.map(
        lambda part, zero: jnp.broadcast_to(jnp.asarray(zero, part.dtype), part.shape),
        shard,
        identity,
    )

    def entering_lap(k, before):
        at = peers - 1 - k
        reached = at > position
        new = combine(
            before, jax.tree.map(lambda part, own: part[at].astype(own.dtype), everything, shard)
        )
        return jax.tree.map(lambda a, b: jnp.where(reached, a, b), new, before)

    return lax.fori_loop(0, peers, entering_lap, start)


def conv_acts(x_ext, bc_ext, dt_raw, conv_x, conv_x_b, conv_bc, conv_bc_b, dt_bias, a_log):
    span_len = dt_raw.shape[0]
    batch_size = dt_raw.shape[1]
    head_count = dt_raw.shape[2]
    tap_count = conv_x.shape[0]
    x_conv = conv_x_b + conv_x[0] * x_ext[0:span_len]
    bc_conv = conv_bc_b + conv_bc[0] * bc_ext[0:span_len]
    for k in range(1, tap_count):
        x_conv = x_conv + conv_x[k] * x_ext[k : k + span_len]
        bc_conv = bc_conv + conv_bc[k] * bc_ext[k : k + span_len]
    x_full = jax.nn.silu(x_conv)
    bc_full = jax.nn.silu(bc_conv)
    group_count = span_len // L
    head_dim = x_full.shape[2] // head_count
    state_size = bc_full.shape[3]
    x_act = x_full.reshape(group_count, L, batch_size, head_count, head_dim)
    b_rows = bc_full[:, :, 0].reshape(group_count, L, batch_size, state_size)
    c_rows = bc_full[:, :, 1].reshape(group_count, L, batch_size, state_size)
    time_step = jax.nn.softplus(dt_raw + dt_bias).reshape(group_count, L, batch_size, head_count)
    cum_decay = jnp.cumsum(time_step * -jnp.exp(a_log), axis=1)
    return (x_act, b_rows, c_rows, time_step, cum_decay)


def group_states(x_act, b_rows, time_step, cum_decay):
    last_decay = cum_decay[:, -1]
    weights = jnp.exp(last_decay[:, None] - cum_decay) * time_step
    weighted = weights[..., None] * x_act
    local_states = jnp.einsum("clbhp,clbn->cbhpn", weighted, b_rows, precision=highest)
    group_decay = jnp.exp(last_decay)
    running = jnp.zeros_like(local_states[0])
    entering = []
    for index in range(local_states.shape[0]):
        entering.append(running)
        running = group_decay[index][..., None, None] * running + local_states[index]
    return (jnp.stack(entering), running, jnp.exp(jnp.sum(last_decay, axis=0)))


def group_output(x_act, b_rows, c_rows, time_step, cum_decay, d_skip, entering, state_in):
    scores = jnp.einsum("ctbn,csbn->ctsb", c_rows, b_rows, precision=highest)
    length = cum_decay.shape[1]
    causal = (jnp.arange(length)[:, None] >= jnp.arange(length)[None, :])[None, :, :, None, None]
    gaps = cum_decay[:, :, None] - cum_decay[:, None, :]
    lower = jnp.where(causal, jnp.exp(jnp.where(causal, gaps, 0.0)), 0.0)
    mixing = scores[..., None] * lower * time_step[:, None]
    intra = jnp.einsum("ctsbh,csbhp->ctbhp", mixing, x_act, precision=highest)
    last_decay = cum_decay[:, -1]
    before = jnp.exp(jnp.cumsum(last_decay, axis=0) - last_decay)
    states = entering + before[..., None, None] * state_in[None]
    inter = jnp.exp(cum_decay)[..., None] * jnp.einsum(
        "ctbn,cbhpn->ctbhp", c_rows, states, precision=highest
    )
    total = intra + inter + d_skip[:, None] * x_act
    shape = x_act.shape
    return total.reshape(shape[0] * shape[1], shape[2], shape[3] * shape[4])


def carry_forward(earlier, later):
    return (earlier[0] * later[0], later[0][..., None, None] * earlier[1] + later[1])


def carry_backward(earlier, later):
    return (later[0] * earlier[0], later[1] + later[0][..., None, None] * earlier[1])


def spread_out(local, rank, axis, count):
    shape = list(local.shape)
    shape[axis] = shape[axis] * count
    full = jnp.zeros(tuple(shape), jnp.float32)
    return lax.dynamic_update_slice_in_dim(full, local, rank * local.shape[axis], axis)


def take_back(summed, rank, axis, length):
    return lax.dynamic_slice_in_dim(summed, rank * length, length, axis)


def shards(
    block_input,
    gain_in,
    w_zx,
    w_bc,
    w_dt,
    conv_x,
    conv_x_b,
    conv_bc,
    conv_bc_b,
    dt_bias,
    a_log,
    d_skip,
    gain_norm,
    w_out,
    cotangent,
):
    rows_dev = block_input.shape[0]
    tensor_count = lax.axis_size("tensor")
    tensor_rank = lax.axis_index("tensor")
    span_len = rows_dev * tensor_count
    tap_count = conv_x.shape[0]
    inner = gain_norm.shape[0]
    inner_total = inner * tensor_count
    width = gain_in.shape[0]
    acc_zx = jnp.zeros((width, 2, inner), jnp.float32)
    acc_dt = jnp.zeros((width, dt_bias.shape[0]), jnp.float32)
    acc_bc = jnp.zeros((width,) + w_bc.shape[1:], jnp.float32)
    acc_out = jnp.zeros((width, inner), jnp.float32)
    small_acc = [
        jnp.zeros(conv_x.shape, jnp.float32),
        jnp.zeros(conv_x_b.shape, jnp.float32),
        jnp.zeros(conv_bc.shape, jnp.float32),
        jnp.zeros(conv_bc_b.shape, jnp.float32),
        jnp.zeros(dt_bias.shape, jnp.float32),
        jnp.zeros(a_log.shape, jnp.float32),
        jnp.zeros(d_skip.shape, jnp.float32),
        jnp.zeros(gain_norm.shape, jnp.float32),
    ]
    acc_gain_in = jnp.zeros(gain_in.shape, jnp.float32)
    results = []
    input_grads = []
    for step in range(MICRO):
        full = (
            lax.all_gather(w_zx, ("dp", "seq"), axis=0, tiled=True),
            lax.all_gather(w_dt, ("dp", "seq"), axis=0, tiled=True),
            lax.all_gather(w_bc, ("dp", "seq"), axis=0, tiled=True),
            lax.all_gather(w_out, ("dp", "seq"), axis=0, tiled=True),
        )
        wide = None
        current, wide = (full, wide)
        full_zx, full_dt, full_bc, full_out = current
        u_rows = block_input[:, step * SEQ_MB : (step + 1) * SEQ_MB]
        flat_in = u_rows.astype(jnp.float32)
        inv_in = lax.rsqrt(jnp.mean(flat_in * flat_in, -1, keepdims=True) + epsilon)
        base = flat_in * inv_in
        normed_rows = (base * gain_in).astype(jnp.bfloat16)
        normed = lax.all_gather(normed_rows, "tensor", axis=0, tiled=True)
        proj = jnp.einsum("tbd,dgk->tbgk", normed, full_zx, preferred_element_type=jnp.float32)
        gate_in = proj[:, :, 0]
        x_pre = proj[:, :, 1]
        bc_pre = jnp.einsum("tbd,dgn->tbgn", normed, full_bc, preferred_element_type=jnp.float32)
        dt_raw = jnp.einsum("tbd,dh->tbh", normed, full_dt, preferred_element_type=jnp.float32)
        tails = shifted(
            (x_pre[span_len - tap_count + 1 :], bc_pre[span_len - tap_count + 1 :]), "seq", 1
        )
        x_ext = jnp.concatenate([tails[0], x_pre], 0)
        bc_ext = jnp.concatenate([tails[1], bc_pre], 0)
        acts, pull_acts = jax.vjp(
            conv_acts, x_ext, bc_ext, dt_raw, conv_x, conv_x_b, conv_bc, conv_bc_b, dt_bias, a_log
        )
        x_act, b_rows, c_rows, time_step, cum_decay = acts
        state_out, pull_states = jax.vjp(group_states, x_act, b_rows, time_step, cum_decay)
        entering, local_state, decay = state_out
        prefix = prefix_2(
            (decay, local_state),
            "seq",
            carry_forward,
            (jnp.ones_like(decay), jnp.zeros_like(local_state)),
        )
        state_in = prefix[1]
        mixed, pull_out = jax.vjp(
            group_output, x_act, b_rows, c_rows, time_step, cum_decay, d_skip, entering, state_in
        )
        gate_act = jax.nn.silu(gate_in)
        gated = mixed * gate_act
        square_sum = lax.psum(jnp.sum(gated * gated, -1), "tensor")
        inv_norm = lax.rsqrt(square_sum / inner_total + epsilon)[..., None]
        hidden = (gated * inv_norm * gain_norm).astype(jnp.bfloat16)
        branch = lax.psum_scatter(
            jnp.einsum("tbk,dk->tbd", hidden, full_out, preferred_element_type=jnp.float32).astype(
                jnp.bfloat16
            ),
            "tensor",
            scatter_dimension=0,
            tiled=True,
        ).astype(jnp.float32)
        results.append((flat_in + branch).astype(jnp.bfloat16))
        cot_rows = cotangent[:, step * SEQ_MB : (step + 1) * SEQ_MB]
        cot_span = lax.all_gather(cot_rows, "tensor", axis=0, tiled=True)
        grad_hidden = jnp.einsum(
            "tbd,dk->tbk", cot_span, full_out, preferred_element_type=jnp.float32
        )
        acc_out = acc_out + jnp.einsum(
            "tbd,tbk->dk", cot_span, hidden, preferred_element_type=jnp.float32
        )
        scaled_hidden = grad_hidden * gain_norm
        small_acc[7] = small_acc[7] + jnp.sum(grad_hidden * gated * inv_norm, (0, 1))
        inner_prod = lax.psum(jnp.sum(scaled_hidden * gated, -1), "tensor")
        grad_gated = (
            inv_norm * scaled_hidden - gated * inv_norm**3 * (inner_prod / inner_total)[..., None]
        )
        sigmoid_gate = jax.nn.sigmoid(gate_in)
        grad_mixed = grad_gated * gate_act
        grad_gate = grad_gated * mixed * sigmoid_gate * (1.0 + gate_in * (1.0 - sigmoid_gate))
        out_cots = pull_out(grad_mixed)
        back = entering_2(
            (decay, out_cots[7]),
            "seq",
            carry_backward,
            (jnp.ones_like(decay), jnp.zeros_like(local_state)),
        )
        carried = back[1]
        grad_decay = jnp.sum(carried * state_in, (-2, -1))
        state_cots = pull_states((out_cots[6], carried, grad_decay))
        grad_b_part = out_cots[1] + state_cots[1]
        grad_b, grad_c = lax.psum((grad_b_part, out_cots[2]), "tensor")
        act_cots = pull_acts(
            (
                out_cots[0] + state_cots[0],
                grad_b,
                grad_c,
                out_cots[3] + state_cots[2],
                out_cots[4] + state_cots[3],
            )
        )
        back_tails = shifted(
            (act_cots[0][: tap_count - 1], act_cots[1][: tap_count - 1]), "seq", -1
        )
        grad_x = act_cots[0][tap_count - 1 :].at[span_len - tap_count + 1 :].add(back_tails[0])
        grad_bc = act_cots[1][tap_count - 1 :].at[span_len - tap_count + 1 :].add(back_tails[1])
        cot_gate = grad_gate.astype(jnp.bfloat16)
        cot_x = grad_x.astype(jnp.bfloat16)
        cot_bc = grad_bc.astype(jnp.bfloat16)
        cot_dt = act_cots[2].astype(jnp.bfloat16)
        acc_zx = acc_zx + jnp.stack(
            [
                jnp.einsum("tbd,tbk->dk", normed, cot_gate, preferred_element_type=jnp.float32),
                jnp.einsum("tbd,tbk->dk", normed, cot_x, preferred_element_type=jnp.float32),
            ],
            1,
        )
        acc_bc = acc_bc + jnp.einsum(
            "tbd,tbgn->dgn", normed, cot_bc, preferred_element_type=jnp.float32
        )
        acc_dt = acc_dt + jnp.einsum(
            "tbd,tbh->dh", normed, cot_dt, preferred_element_type=jnp.float32
        )
        for index in range(6):
            small_acc[index] = small_acc[index] + act_cots[3 + index]
        small_acc[6] = small_acc[6] + out_cots[5]
        grad_normed = lax.psum_scatter(
            jnp.einsum("tbk,dk->tbd", cot_gate, full_zx[:, 0], preferred_element_type=jnp.float32)
            + jnp.einsum("tbk,dk->tbd", cot_x, full_zx[:, 1], preferred_element_type=jnp.float32)
            + jnp.einsum("tbh,dh->tbd", cot_dt, full_dt, preferred_element_type=jnp.float32),
            "tensor",
            scatter_dimension=0,
            tiled=True,
        )
        own_bc = lax.dynamic_slice_in_dim(cot_bc, tensor_rank * rows_dev, rows_dev, 0)
        grad_normed = grad_normed + jnp.einsum(
            "tbgn,dgn->tbd", own_bc, full_bc, preferred_element_type=jnp.float32
        )
        scaled = grad_normed * gain_in
        grad_base = inv_in * (scaled - base * jnp.mean(scaled * base, -1, keepdims=True))
        acc_gain_in = acc_gain_in + jnp.sum(grad_normed * base, (0, 1))
        input_grads.append((cot_rows.astype(jnp.float32) + grad_base).astype(jnp.bfloat16))
    grad_zx, grad_dt, grad_wbc, grad_out = (
        lax.psum_scatter(
            acc_zx.astype(jnp.bfloat16), ("dp", "seq"), scatter_dimension=0, tiled=True
        ).astype(jnp.float32),
        lax.psum_scatter(
            acc_dt.astype(jnp.bfloat16), ("dp", "seq"), scatter_dimension=0, tiled=True
        ).astype(jnp.float32),
        lax.psum_scatter(
            acc_bc.astype(jnp.bfloat16), ("dp", "seq"), scatter_dimension=0, tiled=True
        ).astype(jnp.float32),
        lax.psum_scatter(
            acc_out.astype(jnp.bfloat16), ("dp", "seq"), scatter_dimension=0, tiled=True
        ).astype(jnp.float32),
    )
    first_rank = tensor_rank == 0
    summed = lax.psum(
        (
            spread_out(small_acc[0], tensor_rank, 1, tensor_count),
            spread_out(small_acc[1], tensor_rank, 0, tensor_count),
            jnp.where(first_rank, small_acc[2], 0.0),
            jnp.where(first_rank, small_acc[3], 0.0),
            spread_out(small_acc[4], tensor_rank, 0, tensor_count),
            spread_out(small_acc[5], tensor_rank, 0, tensor_count),
            spread_out(small_acc[6], tensor_rank, 0, tensor_count),
            spread_out(small_acc[7], tensor_rank, 0, tensor_count),
            acc_gain_in,
        ),
        ("dp", "seq", "tensor"),
    )
    head_local = dt_bias.shape[0]
    return (
        jnp.concatenate(results, 1),
        jnp.concatenate(input_grads, 1),
        summed[8],
        grad_zx,
        grad_wbc,
        grad_dt,
        take_back(summed[0], tensor_rank, 1, inner),
        take_back(summed[1], tensor_rank, 0, inner),
        summed[2],
        summed[3],
        take_back(summed[4], tensor_rank, 0, head_local),
        take_back(summed[5], tensor_rank, 0, head_local),
        take_back(summed[6], tensor_rank, 0, head_local),
        take_back(summed[7], tensor_rank, 0, inner),
        grad_out,
    )


def solution(mesh):
    return jax.shard_map(
        shards,
        mesh=mesh,
        in_specs=(
            P(("seq", "tensor"), "dp", None),
            P(),
            P(("dp", "seq"), None, "tensor"),
            P(("dp", "seq"), None, None),
            P(("dp", "seq"), "tensor"),
            P(None, "tensor"),
            P("tensor"),
            P(),
            P(),
            P("tensor"),
            P("tensor"),
            P("tensor"),
            P("tensor"),
            P(("dp", "seq"), "tensor"),
            P(("seq", "tensor"), "dp", None),
        ),
        out_specs=(
            P(("seq", "tensor"), "dp", None),
            P(("seq", "tensor"), "dp", None),
            P(),
            P(("dp", "seq"), None, "tensor"),
            P(("dp", "seq"), None, None),
            P(("dp", "seq"), "tensor"),
            P(None, "tensor"),
            P("tensor"),
            P(),
            P(),
            P("tensor"),
            P("tensor"),
            P("tensor"),
            P("tensor"),
            P(("dp", "seq"), "tensor"),
        ),
        check_vma=False,
    )
```

profile of v0, /device:TPU:0, one launch (start us, length us, event | category | flops | bytes accessed | tf_op | source)
XLA Modules:
  0.0 1405.3 jit_solution(6590031289864375515)
XLA Ops:
  23.2 32.4 %all-gather.8 = bf16[8,192,12]{1,2,0:T(8,128)(2,1)S(1)} all-gather(bf16[1,192,12]{1,2,0:T(8,128)(2,1)S(1)} %bitcast.954), channel_id=1, replica_groups=mesh['dp'=2,'seq'=4,'tensor'=4] {'dp','seq'}, dimensions={0}, use_global_device_ids=true | all-gather | bytes 41472 | tf_op jit(solution)/shard_map/all_gather | solution.py:179
  55.8 36.4 %all_gather.66 = bf16[1536,2,128]{2,0,1:T(8,128)(2,1)} all-gather(bf16[192,2,128]{2,0,1:T(8,128)(2,1)S(1)} %copy.544), channel_id=1, replica_groups=mesh['dp'=2,'seq'=4,'tensor'=4] {'dp','seq'}, dimensions={0}, use_global_device_ids=true | all-gather | bytes 884736 | tf_op jit(solution)/shard_map/all_gather | solution.py:180
  122.5 36.5 %all-gather.20.cloned.1.call-done = bf16[1536,2,768]{2,0,1:T(8,128)(2,1)} async-done(((bf16[192,2,768]{2,0,1:T(8,128)(2,1)}), bf16[1536,2,768]{2,0,1:T(8,128)(2,1)}) %all-gather.20.cloned.1.call-update) | async-done | bytes 4718608 | tf_op jit(solution)/shard_map/all_gather | solution.py:178
  159.0 7.2 fusion.144
  222.5 8.9 all-reduce.64
  232.5 9.9 all-reduce.65
  295.0 18.7 %multiply_reduce_fusion.14 = (f32[4,256]{1,0:T(4,128)S(1)}, f32[4,256,1,12,64]{1,4,3,0,2:T(8,128)S(1)}) fusion(f32[4,256,1,12,64]{1,0,4,3,2:T(4,128)} %squeeze.57, f32[4,256,1,12,64]{1,0,4,3,2:T(4,128)} %reshape.1995, f32[12]{0:T(128)S(1)} %copy-done.280, f32[4,12,64,256]{3,2,1,0:T(8,128)S(1)} %fusion.284, f32[4,256,12]{1,2,0:T(8,128)S(1)} %copy-done.137, ...), kind=kOutput, calls=%fused_computation.191 | convolution fusion | flops 2440297472 | bytes 16994352 | tf_op jit(solution)/shard_map/jvp(ctsbh,csbhp->ctbhp)/dot_general | solution.py:103
  326.4 18.7 %multiply_reduce_fusion.15 = (f32[4,256]{1,0:T(4,128)S(1)}, f32[4,256,1,12,64]{1,4,3,0,2:T(8,128)S(1)}) fusion(f32[4,256,1,12,64]{1,0,4,3,2:T(4,128)} %squeeze.51, f32[4,256,1,12,64]{1,0,4,3,2:T(4,128)} %reshape.1983, f32[12]{0:T(128)S(1)} %copy-done.281, f32[4,12,64,256]{3,2,1,0:T(8,128)S(1)} %fusion.287, f32[4,256,12]{1,2,0:T(8,128)S(1)} %copy-done.139, ...), kind=kOutput, calls=%fused_computation.196 | convolution fusion | flops 2440297472 | bytes 16994352 | tf_op jit(solution)/shard_map/jvp(ctsbh,csbhp->ctbhp)/dot_general | solution.py:103
  378.6 12.3 multiply_reduce_fusion.3
  390.9 7.4 all-reduce.61
  399.7 12.6 fusion.56
  482.2 19.4 %all-gather.4 = bf16[48,64,128]{2,1,0:T(8,128)(2,1)} all-gather(bf16[12,64,128]{2,1,0:T(8,128)(2,1)} %get-tuple-element.807), channel_id=6, replica_groups=mesh['dp'=2,'seq'=4,'tensor'=4] {'seq'}, dimensions={0}, use_global_device_ids=true | all-gather | bytes 983040 | tf_op jit(solution)/shard_map/all_gather | solution.py:38
  501.6 10.3 while.66
  522.3 12.2 fusion.52
  549.4 18.4 %all-gather.5 = bf16[48,64,128]{2,1,0:T(8,128)(2,1)} all-gather(bf16[12,64,128]{2,1,0:T(8,128)(2,1)} %get-tuple-element.809), channel_id=7, replica_groups=mesh['dp'=2,'seq'=4,'tensor'=4] {'seq'}, dimensions={0}, use_global_device_ids=true | all-gather | bytes 983040 | tf_op jit(solution)/shard_map/all_gather | solution.py:38
  567.8 10.1 while.67
  584.8 13.1 fusion.117
  601.9 12.2 fusion.51
  624.2 29.6 %fusion.14 = (f32[4,256,12]{1,2,0:T(8,128)}, f32[4,256,12]{1,2,0:T(8,128)}, f32[4,256,12]{1,2,0:T(8,128)}, f32[4,256,256]{2,1,0:T(8,128)S(1)}, f32[4,256,256]{2,...) fusion(f32[4,256,12]{1,2,0:T(8,128)S(1)} %copy-done.178, ...), kind=kOutput, calls=%fused_computation.35 | convolution fusion | flops 2509692928 | bytes 23625728 | tf_op jit(solution)/shard_map/transpose(jvp(ctsbh,csbhp->ctbhp))/dot_general | solution.py:103
  671.4 9.9 reduce-window.34
  681.6 9.9 reduce-window.36
  702.7 44.4 %all-reduce.71.cloned.1.call-done = (f32[1024,1,2,128]{3,0,2,1:T(8,128)}, f32[1024,1,2,128]{3,0,2,1:T(8,128)}) async-done(((f32[1024,1,2,128]{3,0,2,1:T(8,128)}, f32[1024,1,2,128]{3,0,2,1:T(8,128)}), (f32[1024,1,2,128]{3,0,2,1:T(8,128)}, f32[1024,1,2,128]{3,0,2,1:T(8,128)})) %all-reduce.71.cloned.1.call-update) | async-done | bytes 2097168 | tf_op jit(solution)/shard_map/psum | solution.py:260
  769.6 11.5 fusion.99
  781.3 16.1 %multiply_reduce_fusion.6 = (f32[768]{0:T(1024)S(1)}, f32[768]{0:T(1024)S(1)}, f32[768]{0:T(1024)S(1)}, f32[768]{0:T(1024)S(1)}, f32[768]{0:T(1024)S(1)}, /*inde...) fusion(f32[1024,1,768]{2,0,1:T(8,128)} %copy-done.27, ...), kind=kLoop, calls=%fused_computation.180 | loop fusion | flops 33022464 | bytes 31506432 | tf_op jit(solution)/shard_map/transpose(jvp())/reduce_sum | solution.py:67
  806.3 7.4 convolution_bitcast_fusion.3
  883.8 67.4 %reduce-scatter.27.cloned.1.call-done = bf16[192,768]{1,0:T(8,128)(2,1)} async-done(((bf16[1536,768]{1,0:T(8,128)(2,1)}), bf16[192,768]{1,0:T(8,128)(2,1)}) %reduce-scatter.27.cloned.1.call-update) | async-done | bytes 294928
  953.4 96.4 %reduce-scatter.21.cloned.1.call-done = bf16[192,2,768]{2,0,1:T(8,128)(2,1)} async-done(((bf16[1536,2,768]{2,0,1:T(8,128)(2,1)}), bf16[192,2,768]{2,0,1:T(8,128)(2,1)}) %reduce-scatter.21.cloned.1.call-update) | async-done | bytes 589840 | tf_op jit(solution)/shard_map/reduce_scatter | solution.py:312
  1052.5 58.2 %reduce-scatter.17.cloned.1.call-done = f32[256,1,1536]{2,0,1:T(8,128)} async-done(((f32[1024,1,1536]{2,0,1:T(8,128)}), f32[256,1,1536]{2,0,1:T(8,128)}) %reduce-scatter.17.cloned.1.call-update) | async-done | bytes 1572880 | tf_op jit(solution)/shard_map/reduce_scatter | solution.py:295
  1114.0 37.0 %reduce-scatter.13.cloned.1.call-done = bf16[256,1,1536]{2,0,1:T(8,128)(2,1)} async-done(((bf16[1024,1,1536]{2,0,1:T(8,128)(2,1)}), bf16[256,1,1536]{2,0,1:T(8,128)(2,1)}) %reduce-scatter.13.cloned.1.call-update) | async-done | bytes 786448 | tf_op jit(solution)/shard_map/reduce_scatter | solution.py:223
  1151.0 61.3 %reduce-scatter.19.cloned.1.call-done = f32[256,1,1536]{2,0,1:T(8,128)} async-done(((f32[1024,1,1536]{2,0,1:T(8,128)}), f32[256,1,1536]{2,0,1:T(8,128)}) %reduce-scatter.19.cloned.1.call-update) | async-done | bytes 1572880 | tf_op jit(solution)/shard_map/reduce_scatter | solution.py:295
  1218.4 34.1 %reduce-scatter.15.cloned.1.call-done = bf16[256,1,1536]{2,0,1:T(8,128)(2,1)} async-done(((bf16[1024,1,1536]{2,0,1:T(8,128)(2,1)}), bf16[256,1,1536]{2,0,1:T(8,128)(2,1)}) %reduce-scatter.15.cloned.1.call-update) | async-done | bytes 786448 | tf_op jit(solution)/shard_map/reduce_scatter | solution.py:223
  1262.8 124.0 %all-reduce.69.cloned.1.call-done = (f32[1536]{0:T(1024)}, f32[4,3072]{1,0:T(4,128)}, f32[3072]{0:T(1024)}, f32[4,2,128]{2,1,0:T(2,128)}, f32[2,128]{1,0:T(2,128...) async-done(((f32[1536]{0:T(1024)}, f32[4,3072]{1,0:T(4,128)}, f32[3072]{0:T(1024)}, f32[4,2,128]{2,1,0:T(2,128)}, f32[2,128]{1,0:T(2,128)}, ...) | async-done | bytes 85584 | tf_op jit(solution)/shard_map/psum | solution.py:326
  (987 shorter events, 511.0 us)
Async XLA Ops:
  7.2 85.0 %all-gather.18.cloned.1.call-start = ((), (), s32[]{:S(2)}) async-start(), calls=%async_computation.8 | async-start | bytes 3932160 | tf_op jit(solution)/shard_map/all_gather | solution.py:191
  14.3 82.0 %all-gather.24.cloned.1.call-start = ((), (), s32[]{:S(2)}) async-start(), calls=%async_computation.12 | async-start | bytes 3932160 | tf_op jit(solution)/shard_map/all_gather | solution.py:191
  15.1 143.9 %all-gather.20.cloned.1.call-start = ((), (), s32[]{:S(2)}) async-start(), calls=%async_computation.9 | async-start | bytes 5308416 | tf_op jit(solution)/shard_map/all_gather | solution.py:178
  16.1 228.6 %all-gather.22.cloned.1.call-start = ((), (), s32[]{:S(2)}) async-start(), calls=%async_computation.10 | async-start | bytes 2654208 | tf_op jit(solution)/shard_map/all_gather | solution.py:181
  16.6 228.1 %all-gather.28.cloned.1.call-start = ((), (), s32[]{:S(2)}) async-start(), calls=%async_computation.16 | async-start | bytes 3932160 | tf_op jit(solution)/shard_map/all_gather | solution.py:233
  21.9 266.6 %all-gather.32.cloned.1.call-start = ((), (), s32[]{:S(2)}) async-start(), calls=%async_computation.21 | async-start | bytes 1966080 | tf_op jit(solution)/shard_map/all_gather | solution.py:23
  110.6 7.8 collective-permute-start.1
  115.8 3.3 collective-permute-start.3
  166.2 16.1 %collective-permute-start = (f32[3,1,768]{2,0,1:T(4,128)S(1)}, f32[3,1,768]{2,0,1:T(4,128)S(1)}, u32[]{:S(2)}, u32[]{:S(2)}) collective-permute-start(f32[3,1,768]{2,0,1:T(4,128)S(1)} %slice_bitcast_fusion.9), channel_id=1, source_target_pairs={{0,4},{4,8},{8,12},{1,5},{5,9},{9,13},{2,6},{6,10},{10,14},{3,7},{... | collective-permute-start | bytes 27656 | tf_op jit(solution)/shard_map/ppermute | solution.py:18
  174.4 7.9 collective-permute-start.2
  200.0 116.2 %all-gather.30.cloned.1.call-start = ((), (), s32[]{:S(2)}) async-start(), calls=%async_computation.20 | async-start | bytes 1966080 | tf_op jit(solution)/shard_map/all_gather | solution.py:23
  202.3 468.9 %copy-start.169 = (f32[4,12]{1,0:T(4,128)}, f32[4,12]{1,0:T(4,128)S(1)}, u32[]{:S(2)}) copy-start(f32[4,12]{1,0:T(4,128)S(1)} %get-tuple-element.827) | copy-start | bytes 580
  217.6 161.0 %all-gather.26.cloned.1.call-start = ((), (), s32[]{:S(2)}) async-start(), calls=%async_computation.14 | async-start | bytes 3932160 | tf_op jit(solution)/shard_map/all_gather | solution.py:233
  218.7 528.3 %all-reduce.71.cloned.1.call-start = ((), (), s32[]{:S(2)}) async-start(), calls=%async_computation.25 | async-start | bytes 4194304 | tf_op jit(solution)/shard_map/psum | solution.py:260
  695.8 183.7 %reduce-scatter.25.cloned.1.call-start = ((), (), s32[]{:S(2)}) async-start(), calls=%async_computation.22 | async-start | bytes 442368
  702.7 179.5 %reduce-scatter.23.cloned.1.call-start = ((), (), s32[]{:S(2)}) async-start(), calls=%async_computation.19 | async-start | bytes 884736 | tf_op jit(solution)/shard_map/reduce_scatter | solution.py:318
  753.3 5.5 collective-permute-start.5
  756.1 6.1 collective-permute-start.7
  769.4 181.8 %reduce-scatter.27.cloned.1.call-start = ((), (), s32[]{:S(2)}) async-start(), calls=%async_computation.23 | async-start | bytes 2654208
  781.2 268.6 %reduce-scatter.21.cloned.1.call-start = ((), (), s32[]{:S(2)}) async-start(), calls=%async_computation.18 | async-start | bytes 5308416 | tf_op jit(solution)/shard_map/reduce_scatter | solution.py:312
  801.6 23.5 %collective-permute-start.4 = (f32[3,1,768]{2,0,1:T(4,128)S(1)}, f32[3,1,768]{2,0,1:T(4,128)S(1)}, u32[]{:S(2)}, u32[]{:S(2)}) collective-permute-start(f32[3,1,768]{2,0,1:T(4,128)S(1)} %pad_add_fusion.13), channel_id=1, source_target_pairs={{4,0},{8,4},{12,8},{5,1},{9,5},{13,9},{6,2},{10,6},{14,10},{7,3},{... | collective-permute-start | bytes 27656 | tf_op jit(solution)/shard_map/ppermute | solution.py:18
  802.9 23.6 %collective-permute-start.6 = (f32[3,1,768]{2,0,1:T(4,128)S(1)}, f32[3,1,768]{2,0,1:T(4,128)S(1)}, u32[]{:S(2)}, u32[]{:S(2)}) collective-permute-start(f32[3,1,768]{2,0,1:T(4,128)S(1)} %pad_add_fusion.12), channel_id=1, source_target_pairs={{4,0},{8,4},{12,8},{5,1},{9,5},{13,9},{6,2},{10,6},{14,10},{7,3},{... | collective-permute-start | bytes 27656 | tf_op jit(solution)/shard_map/ppermute | solution.py:18
  839.5 271.2 %reduce-scatter.17.cloned.1.call-start = ((), (), s32[]{:S(2)}) async-start(), calls=%async_computation.15 | async-start | bytes 7864320 | tf_op jit(solution)/shard_map/reduce_scatter | solution.py:295
  851.1 299.9 %reduce-scatter.13.cloned.1.call-start = ((), (), s32[]{:S(2)}) async-start(), calls=%async_computation.11 | async-start | bytes 3932160 | tf_op jit(solution)/shard_map/reduce_scatter | solution.py:223
  859.0 353.3 %reduce-scatter.19.cloned.1.call-start = ((), (), s32[]{:S(2)}) async-start(), calls=%async_computation.17 | async-start | bytes 7864320 | tf_op jit(solution)/shard_map/reduce_scatter | solution.py:295
  869.7 382.8 %reduce-scatter.15.cloned.1.call-start = ((), (), s32[]{:S(2)}) async-start(), calls=%async_computation.13 | async-start | bytes 3932160 | tf_op jit(solution)/shard_map/reduce_scatter | solution.py:223
  877.6 509.1 %all-reduce.69.cloned.1.call-start = ((), (), s32[]{:S(2)}) async-start(), calls=%async_computation.24 | async-start | bytes 177152 | tf_op jit(solution)/shard_map/psum | solution.py:326
  878.7 235.3 %copy-start.164 = (f32[4,3072]{1,0:T(4,128)}, f32[4,3072]{1,0:T(4,128)S(1)}, u32[]{:S(2)}) copy-start(f32[4,3072]{1,0:T(4,128)S(1)} %add_dynamic-update-slice_fusion) | copy-start | bytes 147460
  878.8 235.2 %copy-start.273 = (f32[48]{0:T(128)}, f32[48]{0:T(128)S(1)}, u32[]{:S(2)}) copy-start(f32[48]{0:T(128)S(1)} %add_dynamic-update-slice_fusion.3) | copy-start | bytes 580
  878.9 235.1 %copy-start.274 = (f32[48]{0:T(128)}, f32[48]{0:T(128)S(1)}, u32[]{:S(2)}) copy-start(f32[48]{0:T(128)S(1)} %add_dynamic-update-slice_fusion.4) | copy-start | bytes 580
  953.4 258.9 %copy-start.66 = (bf16[256,1,1536]{2,0,1:T(8,128)(2,1)S(1)}, bf16[256,1,1536]{2,0,1:T(8,128)(2,1)}, u32[]{:S(2)}) copy-start(bf16[256,1,1536]{2,0,1:T(8,128)(2,1)} %copy-done.65) | copy-start | bytes 2359300
  953.4 258.9 %copy-start.219 = (f32[256]{0:T(256)S(1)}, f32[256]{0:T(256)}, u32[]{:S(2)}) copy-start(f32[256]{0:T(256)} %copy-done.218) | copy-start | bytes 3076
  (287 other events, 4162.4 us)
Sparse Core Ops, SparseCore 0:
  14.5 31.2 all-gather.17
  47.9 28.4 all-gather.23
  79.1 79.7 all-gather.19
  160.9 50.1 all-gather.21
  212.5 27.0 all-gather.27
  241.0 37.1 all-gather.31
  280.4 35.8 all-gather.29
  317.8 27.3 all-gather.25
  695.9 51.1 all-reduce.70
  750.7 62.2 reduce-scatter.24
  817.0 62.2 reduce-scatter.22
  882.6 68.6 reduce-scatter.26
  954.9 94.8 reduce-scatter.20
  1052.2 58.4 reduce-scatter.16
  1113.1 37.8 reduce-scatter.12
  1153.4 58.8 reduce-scatter.18
  1214.7 37.8 reduce-scatter.14
  1260.0 126.7 all-reduce.68
where the time goes:
time: 1420 us; the launch traced here: 1410 us
  waiting for transfers between devices  565 us (40%)
  matrix products  292 us (21%)
  local copies, waits for them, and re-layouts  202 us (14%)
  other arithmetic  170 us (12%)
  blocking collectives  139 us (10%)
  between operations  19.3 us (1%)
  starting transfers between devices  19.1 us (1%)
    psum x1, waiting for transfers between devices, shards(): lax.psum((spread_out(small_acc[0], tensor_rank, 1, tensor_count), spread_...  124 us
    reduce_scatter x2, waiting for transfers between devices, shards(): lax.psum_scatter(jnp.einsum('tbk,dk->tbd', cot_gate, full_zx[:, 0], prefe...  120 us
    dot_general x6, matrix products, group_output(): intra = jnp.einsum('ctsbh,csbhp->ctbhp', mixing, x_act, precision=highest)  105 us
    reduce_scatter x1, waiting for transfers between devices, shards(): lax.psum_scatter(acc_zx.astype(jnp.bfloat16), ('dp', 'seq'), scatter_dime...  96.4 us
    reduce_scatter x2, waiting for transfers between devices, shards(): lax.psum_scatter(jnp.einsum('tbk,dk->tbd', hidden, full_out, preferred_el...  71.1 us
    unnamed x20, waiting for transfers between devices  68.9 us
    psum x1, waiting for transfers between devices, shards(): grad_b, grad_c = lax.psum((grad_b_part, out_cots[2]), 'tensor')  44.4 us
    unnamed x617, local copies, waits for them, and re-layouts  44.2 us
  transfers between devices with their start and end apart: 26, of which 13 were waited for; matrix products, arithmetic and copies ran while one was open for 26% of the time, Pallas kernels for 0%

commit v1 on v0

v1 whole, which is shorter than its diff:
```python
import functools

import jax
import jax.numpy as jnp
from jax import lax
from jax.experimental import pallas as pl
from jax.experimental.pallas import tpu as pltpu
from jax.sharding import PartitionSpec as P

L = 256
HD = 64
LANES = 128
EPS = 1e-05
F32 = jnp.float32
BF = jnp.bfloat16
MESH = pl.DeviceIdType.MESH
VMEM_LIMIT = 60 * 1024 * 1024
NEG = -1e30


def dot(a, b):
    return jnp.dot(a, b, preferred_element_type=F32)


def dot_nt(a, b):
    return lax.dot_general(a, b, (((1,), (1,)), ((), ())), preferred_element_type=F32)


def split(v):
    hi = v.astype(BF)
    return hi, (v - hi.astype(F32)).astype(BF)


def dot_split(mat, v):
    hi, lo = split(v)
    return dot(mat, hi) + dot(mat, lo)


def split_dot(v, mat):
    hi, lo = split(v)
    return dot(hi, mat) + dot(lo, mat)


def iota(shape, axis):
    return lax.broadcasted_iota(jnp.int32, shape, axis)


def pair_of(col, i, low):
    rows = col.shape[0]
    a = jnp.broadcast_to(col[:, 2 * i : 2 * i + 1], (rows, LANES))
    b = jnp.broadcast_to(col[:, 2 * i + 1 : 2 * i + 2], (rows, LANES))
    return jnp.where(low[:rows], a, b)


def segments(i):
    r, c = iota((LANES, LANES), 0), iota((LANES, LANES), 1)
    return jnp.where(c == 2 * i + jnp.where(r >= HD, 1, 0), 1.0, 0.0).astype(BF)


def sigmoid(v):
    return 1.0 / (1.0 + jnp.exp(-v))


def softplus(z):
    return jnp.maximum(z, 0.0) + jnp.log1p(jnp.exp(-jnp.abs(z)))


def acts_kernel(
    pairs,
    x_ref,
    bc_ref,
    dt_ref,
    halo_ref,
    cx_ref,
    cbc_ref,
    small_ref,
    xa_ref,
    dsx_ref,
    bca_ref,
    dsbc_ref,
    time_ref,
    cum_ref,
    state_ref,
    tot_ref,
    ext_x,
    ext_bc,
):
    j = pl.program_id(1)
    width = pairs * LANES

    @pl.when(j == 0)
    def _():
        ext_x[0:8, :] = halo_ref[0, :, 0:width]
        ext_bc[0:8, :] = halo_ref[0, :, width : width + 2 * LANES]
        state_ref[...] = jnp.zeros_like(state_ref)
        tot_ref[...] = jnp.zeros_like(tot_ref)

    ext_x[8 : 8 + L, :] = x_ref[0]
    ext_bc[8 : 8 + L, :] = bc_ref[0]
    low = iota((L, LANES), 1) < HD
    z = dt_ref[0] + small_ref[0:1, :]
    step = softplus(z)
    tri = jnp.where(iota((L, L), 0) >= iota((L, L), 1), 1.0, 0.0).astype(BF)
    rate = step * small_ref[1:2, :]
    r1 = rate.astype(BF)
    rest = rate - r1.astype(F32)
    r2 = rest.astype(BF)
    r3 = (rest - r2.astype(F32)).astype(BF)
    cum = dot(tri, r1) + dot(tri, r2) + dot(tri, r3)
    time_ref[0] = step
    cum_ref[0] = cum
    last = cum[L - 1 : L, :]
    tot_ref[0] = tot_ref[0] + jnp.broadcast_to(last, (8, LANES))
    decay = jnp.exp(last)
    weight = jnp.exp(last - cum) * step

    def act(ext, taps, at):
        v = taps[4:5, at] + taps[0:1, at] * ext[5 : 5 + L, at]
        for k in range(1, 4):
            v = v + taps[k : k + 1, at] * ext[5 + k : 5 + k + L, at]
        s = sigmoid(v)
        a = v * s
        return a, s * (1.0 + v * (1.0 - s))

    b_t = None
    for i in range(2):
        at = slice(i * LANES, (i + 1) * LANES)
        a, d = act(ext_bc, cbc_ref, at)
        bca_ref[0, :, at] = a
        dsbc_ref[0, :, at] = d.astype(BF)
        if i == 0:
            b_t = a.T.astype(BF)
    for i in range(pairs):
        at = slice(i * LANES, (i + 1) * LANES)
        a, d = act(ext_x, cx_ref, at)
        xa_ref[0, :, at] = a
        dsx_ref[0, :, at] = d.astype(BF)
        wx = (a * pair_of(weight, i, low)).astype(BF)
        state_ref[0, :, at] = state_ref[0, :, at] * pair_of(decay, i, low) + dot(b_t, wx)
    ext_x[0:8, :] = ext_x[L : L + 8, :]
    ext_bc[0:8, :] = ext_bc[L : L + 8, :]


def forward_kernel(
    pairs,
    x_ref,
    bc_ref,
    time_ref,
    cum_ref,
    gate_ref,
    gh_ref,
    in_ref,
    chan_ref,
    mixed_ref,
    ent_ref,
    aft_ref,
    stat_ref,
    state,
):
    j = pl.program_id(1)

    @pl.when(j == 0)
    def _():
        state[...] = in_ref[0]

    low = iota((L, LANES), 1) < HD
    b_t, b_lo = split(bc_ref[0, :, 0:LANES].T)
    c, c_lo = split(bc_ref[0, :, LANES : 2 * LANES])
    scores = dot(c, b_t) + (dot(c, b_lo) + dot(c_lo, b_t))
    step, cum = time_ref[0], cum_ref[0]
    cum_t = cum.T
    last = cum[L - 1 : L, :]
    decay = jnp.exp(last)
    grow = jnp.exp(cum)
    weight = jnp.exp(last - cum) * step
    half = L // 2
    mask = jnp.where(iota((half, half), 0) >= iota((half, half), 1), 0.0, NEG)
    squares = jnp.zeros((L, LANES), F32)
    inner = jnp.zeros((L, LANES), F32)
    for i in range(pairs):
        at = slice(i * LANES, (i + 1) * LANES)
        x = x_ref[0, :, at]
        xdt = x * pair_of(step, i, low)
        xdt_b, xdt_lo = split(xdt)
        old = state[:, at]
        old_b, old_lo = split(old)
        ent_ref[0, 0, :, at] = old_b
        y = pair_of(grow, i, low) * (dot(c, old_b) + dot(c, old_lo))
        new = old * pair_of(decay, i, low) + dot_split(b_t, x * pair_of(weight, i, low))
        state[:, at] = new
        aft_ref[0, 0, :, at] = new
        tops = jnp.zeros((half, LANES), F32)
        bots = jnp.zeros((half, LANES), F32)
        zero = jnp.zeros_like(xdt_b)
        for s in range(2):
            h = 2 * i + s
            xm = jnp.where(low, xdt_b, zero) if s == 0 else jnp.where(low, zero, xdt_b)
            xl = jnp.where(low, xdt_lo, zero) if s == 0 else jnp.where(low, zero, xdt_lo)
            top = jnp.exp(cum[:half, h : h + 1] - cum_t[h : h + 1, :half] + mask)
            mix = (top * scores[:half, :half]).astype(BF)
            tops = tops + (dot(mix, xm[:half]) + dot(mix, xl[:half]))
            left = jnp.exp(cum[half:, h : h + 1] - cum_t[h : h + 1, :half])
            right = jnp.exp(cum[half:, h : h + 1] - cum_t[h : h + 1, half:] + mask)
            mix = jnp.concatenate(
                [
                    (left * scores[half:, :half]).astype(BF),
                    (right * scores[half:, half:]).astype(BF),
                ],
                axis=1,
            )
            bots = bots + (dot(mix, xm) + dot(mix, xl))
        y = y + jnp.concatenate([tops, bots], axis=0)
        mixed = y + chan_ref[0:1, at] * x
        mixed_ref[0, :, at] = mixed
        gate = gate_ref[0, :, at]
        gated = mixed * (gate * sigmoid(gate))
        squares = squares + gated * gated
        inner = inner + gated * (gh_ref[0, :, at] * chan_ref[1:2, at])
    lane = iota((L, LANES), 1)
    both = jnp.where(
        lane == 0,
        jnp.sum(squares, axis=1, keepdims=True),
        jnp.where(lane == 1, jnp.sum(inner, axis=1, keepdims=True), 0.0),
    )
    stat_ref[0] = both.T[0:2, :]


def gating_kernel(
    pairs,
    total,
    x_ref,
    bc_ref,
    cum_ref,
    gate_ref,
    gh_ref,
    mixed_ref,
    stat_ref,
    chan_ref,
    grad_ref,
    cgate_ref,
    hidden_ref,
    ds_ref,
    sums_ref,
    before,
):
    n, j = pl.program_id(0), pl.program_id(1)

    @pl.when(j == 0)
    def _():
        before[...] = jnp.zeros_like(before)
        ds_ref[...] = jnp.zeros_like(ds_ref)

    @pl.when((j == 0) & (n == 0))
    def _():
        sums_ref[...] = jnp.zeros_like(sums_ref)

    low = iota((L, LANES), 1) < HD
    rows = iota((LANES, L), 0)
    stat = jnp.where(
        rows == 0,
        jnp.broadcast_to(stat_ref[0, 0:1, :], (LANES, L)),
        jnp.broadcast_to(stat_ref[0, 1:2, :], (LANES, L)),
    ).T
    inv = lax.rsqrt(stat[:, 0:1] * (1.0 / total) + EPS)
    back = inv * inv * inv * (stat[:, 1:2] * (1.0 / total))
    inv = jnp.broadcast_to(inv, (L, LANES))
    back = jnp.broadcast_to(back, (L, LANES))
    cum = cum_ref[0]
    grow = jnp.exp(cum + before[0:1, :])
    before[...] = before[...] + jnp.broadcast_to(cum[L - 1 : L, :], before.shape)
    c_t = bc_ref[0, :, LANES : 2 * LANES].T.astype(BF)
    for i in range(pairs):
        at = slice(i * LANES, (i + 1) * LANES)
        x = x_ref[0, :, at]
        gate = gate_ref[0, :, at]
        mixed = mixed_ref[0, :, at]
        gh = gh_ref[0, :, at]
        gain = chan_ref[1:2, at]
        sig = sigmoid(gate)
        act = gate * sig
        gated = mixed * act
        normal = gated * inv
        hidden_ref[0, :, at] = (normal * gain).astype(BF)
        grad_gated = inv * (gh * gain) - gated * back
        grad = grad_gated * act
        grad_ref[0, :, at] = grad
        cgate_ref[0, :, at] = (grad_gated * mixed * sig * (1.0 + gate * (1.0 - sig))).astype(BF)
        ds_ref[0, :, at] = ds_ref[0, :, at] + dot(
            c_t, (grad * pair_of(grow, i, low)).astype(BF)
        )
        sums_ref[0:1, at] = sums_ref[0:1, at] + jnp.sum(gh * normal, axis=0, keepdims=True)
        sums_ref[1:2, at] = sums_ref[1:2, at] + jnp.sum(grad * x, axis=0, keepdims=True)


def backward_kernel(
    pairs,
    grad_ref,
    cgate_ref,
    x_ref,
    dsx_ref,
    bc_ref,
    dsbc_ref,
    time_ref,
    cum_ref,
    ent_ref,
    aft_ref,
    mixed_ref,
    px_ref,
    pbc_ref,
    pdt_ref,
    halo_ref,
    carried_ref,
    chan_ref,
    cx_ref,
    cbc_ref,
    small_ref,
    cot_ref,
    tail_ref,
    sx_ref,
    sbc_ref,
    sdt_ref,
    state,
    ext_x,
    ext_bc,
):
    n, g = pl.program_id(0), pl.program_id(1)
    final = pl.num_programs(1) - 1
    width = pairs * LANES

    @pl.when(g == 0)
    def _():
        state[...] = carried_ref[0]
        ext_x[L : L + 8, :] = jnp.zeros((8, width), F32)
        ext_bc[L : L + 8, :] = jnp.zeros((8, 2 * LANES), F32)

    @pl.when((g == 0) & (n == 0))
    def _():
        sx_ref[...] = jnp.zeros_like(sx_ref)
        sbc_ref[...] = jnp.zeros_like(sbc_ref)
        sdt_ref[...] = jnp.zeros_like(sdt_ref)

    low = iota((L, LANES), 1) < HD
    b, b_lo = split(bc_ref[0, :, 0:LANES])
    c_full = bc_ref[0, :, LANES : 2 * LANES]
    c = c_full.astype(BF)
    c_t, c_lo = split(c_full.T)
    scores_t = dot(b, c_t) + (dot(b, c_lo) + dot(b_lo, c_t))
    step, cum = time_ref[0], cum_ref[0]
    cum_t = cum.T
    last = cum[L - 1 : L, :]
    decay = jnp.exp(last)
    grow = jnp.exp(cum)
    fade = jnp.exp(last - cum)
    half = L // 2
    mask = jnp.where(iota((half, half), 1) >= iota((half, half), 0), 0.0, NEG)
    grad_b = jnp.zeros((L, LANES), F32)
    grad_c = jnp.zeros((L, LANES), F32)
    ds_a = jnp.zeros((half, half), F32)
    ds_b = jnp.zeros((half, half), F32)
    ds_d = jnp.zeros((half, half), F32)
    dcum = jnp.zeros((L, LANES), F32)
    cols = jnp.zeros((L, LANES), F32)
    dlast = jnp.zeros((8, LANES), F32)

    for i in range(pairs):
        at = slice(i * LANES, (i + 1) * LANES)
        seg = segments(i)
        x = x_ref[0, :, at]
        dt_e = pair_of(step, i, low)
        fade_e = pair_of(fade, i, low)
        xdt = x * dt_e
        xdt_b = xdt.astype(BF)
        gm = grad_ref[0, :, at]
        gm_b, gm_lo = split(gm)
        grow_g, grow_lo = split(gm * pair_of(grow, i, low))
        ds_old = state[:, at]
        ds_old_b, ds_old_lo = split(ds_old)
        dxdt = fade_e * (dot(b, ds_old_b) + dot(b, ds_old_lo))
        grad_b = grad_b + dot_nt((xdt * fade_e).astype(BF), ds_old_b)
        grad_c = grad_c + dot_nt(grow_g, ent_ref[0, 0, :, at])
        lasts = jnp.sum(aft_ref[0, 0, :, at] * ds_old, axis=0, keepdims=True)
        dlast = dlast + split_dot(jnp.broadcast_to(lasts, (8, LANES)), seg)
        state[:, at] = ds_old * pair_of(decay, i, low) + (dot(c_t, grow_g) + dot(c_t, grow_lo))
        zero = jnp.zeros_like(xdt_b)
        tops = jnp.zeros((half, LANES), F32)
        bots = jnp.zeros((half, LANES), F32)
        for s in range(2):
            h = 2 * i + s
            xm = jnp.where(low, xdt_b, zero) if s == 0 else jnp.where(low, zero, xdt_b)
            gs = jnp.where(low, gm_b, zero) if s == 0 else jnp.where(low, zero, gm_b)
            gl = jnp.where(low, gm_lo, zero) if s == 0 else jnp.where(low, zero, gm_lo)
            row, col = cum_t[h : h + 1, :], cum[:, h : h + 1]
            low_a = jnp.exp(row[:, :half] - col[:half] + mask)
            low_b = jnp.exp(row[:, half:] - col[:half])
            low_d = jnp.exp(row[:, half:] - col[half:] + mask)
            dm_top = dot_nt(xm[:half], gm_b)
            dm_bot = dot_nt(xm[half:], gm_b[half:])
            ds_a = ds_a + dm_top[:, :half] * low_a
            ds_b = ds_b + dm_top[:, half:] * low_b
            ds_d = ds_d + dm_bot * low_d
            mix = jnp.concatenate(
                [
                    (low_a * scores_t[:half, :half]).astype(BF),
                    (low_b * scores_t[:half, half:]).astype(BF),
                ],
                axis=1,
            )
            tops = tops + (dot(mix, gs) + dot(mix, gl))
            mix = (low_d * scores_t[half:, half:]).astype(BF)
            bots = bots + (dot(mix, gs[half:]) + dot(mix, gl[half:]))
        dxdt = dxdt + jnp.concatenate([tops, bots], axis=0)
        skip = chan_ref[0:1, at]
        dcum = dcum + split_dot(gm * (mixed_ref[0, :, at] - skip * x), seg)
        cols = cols + split_dot(xdt * dxdt, seg)
        gx = (dt_e * dxdt + skip * gm) * dsx_ref[0, :, at].astype(F32)
        ext_x[0:L, at] = gx
        px = px_ref[0, :, at]
        cot = cx_ref[3:4, at] * gx
        sx_ref[3:4, at] = sx_ref[3:4, at] + jnp.sum(px * gx, axis=0, keepdims=True)
        sx_ref[4:5, at] = sx_ref[4:5, at] + jnp.sum(gx, axis=0, keepdims=True)
        for k in range(3):
            moved = ext_x[3 - k : 3 - k + L, at]
            cot = cot + cx_ref[k : k + 1, at] * moved
            sx_ref[k : k + 1, at] = sx_ref[k : k + 1, at] + jnp.sum(
                px * moved, axis=0, keepdims=True
            )
        cot_ref[0, :, at] = cgate_ref[0, :, at]
        cot_ref[0, :, width + i * LANES : width + (i + 1) * LANES] = cot.astype(BF)

    zero = jnp.zeros((half, half), F32)
    ds_t = jnp.concatenate(
        [jnp.concatenate([ds_a, ds_b], axis=1), jnp.concatenate([zero, ds_d], axis=1)], axis=0
    )
    grad_b = grad_b + dot(ds_t.astype(BF), c)
    grad_c = grad_c + dot(ds_t.T.astype(BF), b)
    for i, part in ((0, grad_b), (1, grad_c)):
        at = slice(i * LANES, (i + 1) * LANES)
        gb = part * dsbc_ref[0, :, at].astype(F32)
        ext_bc[0:L, at] = gb
        pb = pbc_ref[0, :, at]
        cot = cbc_ref[3:4, at] * gb
        sbc_ref[3:4, at] = sbc_ref[3:4, at] + jnp.sum(pb * gb, axis=0, keepdims=True)
        sbc_ref[4:5, at] = sbc_ref[4:5, at] + jnp.sum(gb, axis=0, keepdims=True)
        for k in range(3):
            moved = ext_bc[3 - k : 3 - k + L, at]
            cot = cot + cbc_ref[k : k + 1, at] * moved
            sbc_ref[k : k + 1, at] = sbc_ref[k : k + 1, at] + jnp.sum(
                pb * moved, axis=0, keepdims=True
            )
        cot_ref[0, :, 2 * width + i * LANES : 2 * width + (i + 1) * LANES] = cot.astype(BF)

    upper = jnp.where(iota((L, L), 1) >= iota((L, L), 0), 1.0, 0.0).astype(BF)
    drate = dot_split(upper, dcum - cols) + dlast[0:1, :]
    z = pdt_ref[0] + small_ref[0:1, :]
    sig = sigmoid(z)
    ratio = jnp.where(z < -15.0, 1.0, sig / jnp.where(z < -15.0, 1.0, step))
    dz = cols * ratio + drate * small_ref[1:2, :] * sig
    cot_ref[0, :, 2 * width + 2 * LANES : 2 * width + 3 * LANES] = dz.astype(BF)
    sdt_ref[0:1, :] = sdt_ref[0:1, :] + jnp.sum(dz, axis=0, keepdims=True)
    sdt_ref[1:2, :] = sdt_ref[1:2, :] + jnp.sum(
        drate * step * small_ref[1:2, :], axis=0, keepdims=True
    )

    @pl.when(g == final)
    def _():
        for ext, taps, sums, first, wide in (
            (ext_x, cx_ref, sx_ref, 0, width),
            (ext_bc, cbc_ref, sbc_ref, width, 2 * LANES),
        ):
            both = jnp.concatenate([jnp.zeros((8, wide), F32), ext[0:8, :]], axis=0)
            before = halo_ref[0, :, first : first + wide]
            total = jnp.zeros((8, wide), F32)
            for k in range(3):
                moved = both[3 - k : 11 - k, :]
                total = total + taps[k : k + 1, :] * moved
                sums[k : k + 1, :] = sums[k : k + 1, :] + jnp.sum(
                    before * moved, axis=0, keepdims=True
                )
            tail_ref[0, :, first : first + wide] = total
        tail_ref[0, :, width + 2 * LANES :] = jnp.zeros((8, LANES), F32)

    ext_x[L : L + 8, :] = ext_x[0:8, :]
    ext_bc[L : L + 8, :] = ext_bc[0:8, :]


def tensor_peers():
    me = lax.axis_index("tensor")
    chip, core = me // 2, lax.rem(me, 2)
    partner = chip * 2 + (1 - core)
    across = (1 - chip) * 2 + core
    return me, chip, core, partner, across


def greet(partner, across):
    barrier = pltpu.get_barrier_semaphore()
    for peer in (partner, across):
        pl.semaphore_signal(barrier, inc=1, device_id={"tensor": peer}, device_id_type=MESH)
    pl.semaphore_wait(barrier, 2)


def gather_kernel(cuts, count, *refs):
    ins, outs = refs[:count], refs[count : 2 * count]
    own_sem, near_s, near_r, far_s, far_r, pass_s, pass_r = refs[2 * count :]
    me, chip, core, partner, across = tensor_peers()
    greet(partner, across)
    batch, rows = ins[0].shape[0], ins[0].shape[1]
    piece = rows // cuts

    def remote(src, dst, send, recv, peer):
        return pltpu.make_async_remote_copy(
            src_ref=src,
            dst_ref=dst,
            send_sem=send,
            recv_sem=recv,
            device_id={"tensor": peer},
            device_id_type=MESH,
        )

    todo = []
    at = 0
    for a in range(count):
        for n in range(batch):
            for cut in range(cuts):
                mine = pl.ds(pl.multiple_of(me * rows + cut * piece, piece), piece)
                theirs = pl.ds(pl.multiple_of(across * rows + cut * piece, piece), piece)
                src = ins[a].at[n, cut * piece : (cut + 1) * piece, :]
                far = remote(src, outs[a].at[n, mine, :], far_s.at[at], far_r.at[at], across)
                near = remote(src, outs[a].at[n, mine, :], near_s.at[at], near_r.at[at], partner)
                own = pltpu.make_async_copy(src, outs[a].at[n, mine, :], own_sem.at[at])
                here = outs[a].at[n, theirs, :]
                onward = remote(here, here, pass_s.at[at], pass_r.at[at], partner)
                todo.append((far, near, own, onward))
                at += 1
    for far, near, own, onward in todo:
        far.start()
    for far, near, own, onward in todo:
        near.start()
        own.start()
    for far, near, own, onward in todo:
        far.wait_recv()
        onward.start()
    for far, near, own, onward in todo:
        far.wait_send()
        near.wait()
        own.wait()
        onward.wait()


def gather_tokens(*arrays):
    size = lax.axis_size("tensor")
    if size != 4:
        return [lax.all_gather(a, "tensor", axis=1, tiled=True) for a in arrays]
    batch, rows, width = arrays[0].shape
    count, cuts = len(arrays), 2
    sems = count * batch * cuts
    out = jax.ShapeDtypeStruct((batch, size * rows, width), arrays[0].dtype)
    return pl.pallas_call(
        functools.partial(gather_kernel, cuts, count),
        out_shape=[out] * count,
        in_specs=[pl.BlockSpec(memory_space=pltpu.VMEM)] * count,
        out_specs=[pl.BlockSpec(memory_space=pl.ANY)] * count,
        scratch_shapes=[pltpu.SemaphoreType.DMA((sems,))] * 7,
        compiler_params=pltpu.CompilerParams(
            collective_id=0, has_side_effects=True, vmem_limit_bytes=16 * 1024 * 1024
        ),
        name="gather_tokens",
    )(*arrays)


def scatter_kernel(cuts, in_ref, out_ref, near_buf, far_buf, sum_buf, near_s, near_r, far_s, far_r):
    me, chip, core, partner, across = tensor_peers()
    greet(partner, across)
    batch, rows = out_ref.shape[0], out_ref.shape[1]
    piece = rows // cuts

    def rows_of(owner, cut):
        return pl.ds(pl.multiple_of(owner * rows + cut * piece, piece), piece)

    def remote(src, dst, send, recv, peer):
        return pltpu.make_async_remote_copy(
            src_ref=src,
            dst_ref=dst,
            send_sem=send,
            recv_sem=recv,
            device_id={"tensor": peer},
            device_id_type=MESH,
        )

    near = {}
    for step, target in ((0, (1 - chip) * 2 + (1 - core)), (1, chip * 2 + (1 - core))):
        for n in range(batch):
            for cut in range(cuts):
                at = (step * batch + n) * cuts + cut
                near[step, n, cut] = remote(
                    in_ref.at[n, rows_of(target, cut), :],
                    near_buf.at[at],
                    near_s.at[at],
                    near_r.at[at],
                    partner,
                )
                near[step, n, cut].start()
    far = {}
    for n in range(batch):
        for cut in range(cuts):
            at = n * cuts + cut
            near[0, n, cut].wait_recv()
            sum_buf[at] = (
                in_ref[n, rows_of(across, cut), :].astype(F32) + near_buf[at].astype(F32)
            ).astype(BF)
            far[n, cut] = remote(
                sum_buf.at[at], far_buf.at[at], far_s.at[at], far_r.at[at], across
            )
            far[n, cut].start()
    for n in range(batch):
        for cut in range(cuts):
            at = n * cuts + cut
            near[1, n, cut].wait_recv()
            far[n, cut].wait_recv()
            out_ref[n, cut * piece : (cut + 1) * piece, :] = (
                in_ref[n, rows_of(me, cut), :].astype(F32)
                + near_buf[batch * cuts + at].astype(F32)
                + far_buf[at].astype(F32)
            )
    for key in near:
        near[key].wait_send()
    for key in far:
        far[key].wait_send()


def scatter_tokens(part, ident):
    size = lax.axis_size("tensor")
    if size != 4:
        return lax.psum_scatter(part, "tensor", scatter_dimension=1, tiled=True).astype(F32)
    batch, tokens, width = part.shape
    rows, cuts = tokens // size, 2
    piece = rows // cuts
    return pl.pallas_call(
        functools.partial(scatter_kernel, cuts),
        out_shape=jax.ShapeDtypeStruct((batch, rows, width), F32),
        in_specs=[pl.BlockSpec(memory_space=pltpu.VMEM)],
        out_specs=pl.BlockSpec(memory_space=pltpu.VMEM),
        scratch_shapes=[
            pltpu.VMEM((2 * batch * cuts, piece, width), BF),
            pltpu.VMEM((batch * cuts, piece, width), BF),
            pltpu.VMEM((batch * cuts, piece, width), BF),
            pltpu.SemaphoreType.DMA((2 * batch * cuts,)),
            pltpu.SemaphoreType.DMA((2 * batch * cuts,)),
            pltpu.SemaphoreType.DMA((batch * cuts,)),
            pltpu.SemaphoreType.DMA((batch * cuts,)),
        ],
        compiler_params=pltpu.CompilerParams(
            collective_id=ident, has_side_effects=True, vmem_limit_bytes=40 * 1024 * 1024
        ),
        name="scatter_tokens",
    )(part)


def chain_kernel(by, cuts, own_ref, tot_ref, out_ref, in_buf, send_buf, send_sem, recv_sem):
    me, size = lax.axis_index("seq"), lax.axis_size("seq")
    ahead, behind = me + by, me - by
    has_next = (ahead >= 0) & (ahead < size)
    has_prev = (behind >= 0) & (behind < size)
    barrier = pltpu.get_barrier_semaphore()

    @pl.when(has_next)
    def _():
        pl.semaphore_signal(barrier, inc=1, device_id={"seq": ahead}, device_id_type=MESH)

    @pl.when(has_prev)
    def _():
        pl.semaphore_signal(barrier, inc=1, device_id={"seq": behind}, device_id_type=MESH)

    pl.semaphore_wait(barrier, has_next.astype(jnp.int32) + has_prev.astype(jnp.int32))

    batch, rows = own_ref.shape[0], own_ref.shape[1] // cuts
    copies = []
    for n in range(batch):
        decay = jnp.exp(tot_ref[n, 0:1, :])
        for cut in range(cuts):
            at = n * cuts + cut
            here = slice(cut * rows, (cut + 1) * rows)
            copy = pltpu.make_async_remote_copy(
                src_ref=send_buf.at[at],
                dst_ref=in_buf.at[at],
                send_sem=send_sem.at[at],
                recv_sem=recv_sem.at[at],
                device_id={"seq": ahead},
                device_id_type=MESH,
            )
            copies.append(copy)

            @pl.when(has_prev)
            def _():
                copy.wait_recv()
                out_ref[n, here, :] = in_buf[at].astype(F32)

            @pl.when(jnp.logical_not(has_prev))
            def _():
                out_ref[n, here, :] = jnp.zeros((rows, out_ref.shape[2]), F32)

            @pl.when(has_next)
            def _():
                send_buf[at] = (out_ref[n, here, :] * decay + own_ref[n, here, :]).astype(BF)
                copy.start()

    @pl.when(has_next)
    def _():
        for copy in copies:
            copy.wait_send()


def chain(own, tot, by, ident):
    batch, rows, width = own.shape
    cuts = 4
    return pl.pallas_call(
        functools.partial(chain_kernel, by, cuts),
        out_shape=jax.ShapeDtypeStruct(own.shape, F32),
        in_specs=[pl.BlockSpec(memory_space=pltpu.VMEM)] * 2,
        out_specs=pl.BlockSpec(memory_space=pltpu.VMEM),
        scratch_shapes=[
            pltpu.VMEM((batch * cuts, rows // cuts, width), BF),
            pltpu.VMEM((batch * cuts, rows // cuts, width), BF),
            pltpu.SemaphoreType.DMA((batch * cuts,)),
            pltpu.SemaphoreType.DMA((batch * cuts,)),
        ],
        compiler_params=pltpu.CompilerParams(collective_id=ident, has_side_effects=True),
        name="chain",
    )(own, tot)


def sum_kernel(phases, in_ref, out_ref, *scratch):
    count = len(phases)
    bufs, sends, recvs = scratch[:count], scratch[count : 2 * count], scratch[2 * count :]
    barrier = pltpu.get_barrier_semaphore()
    greeted = 0
    for axis, _ in phases:
        me, size = lax.axis_index(axis), lax.axis_size(axis)
        for d in range(1, size):
            peer = lax.rem(me + d, size)
            pl.semaphore_signal(barrier, inc=1, device_id={axis: peer}, device_id_type=MESH)
            greeted += 1
    pl.semaphore_wait(barrier, greeted)
    out_ref[...] = in_ref[...]
    for p, (axis, first) in enumerate(phases):
        me, size = lax.axis_index(axis), lax.axis_size(axis)
        rows = in_ref.shape[0] - first
        bufs[p][pl.ds(me, 1)] = out_ref[first:, :].reshape(1, rows, LANES)
        copies = []
        for d in range(1, size):
            copies.append(
                pltpu.make_async_remote_copy(
                    src_ref=(in_ref if p == 0 else out_ref).at[pl.ds(first, rows), :],
                    dst_ref=bufs[p].at[me],
                    send_sem=sends[p].at[d - 1],
                    recv_sem=recvs[p].at[d - 1],
                    device_id={axis: lax.rem(me + d, size)},
                    device_id_type=MESH,
                )
            )
            copies[-1].start()
        for copy in copies:
            copy.wait()
        total = bufs[p][0]
        for r in range(1, size):
            total = total + bufs[p][r]
        out_ref[first:, :] = total


def small_sum(value, phases, ident):
    rows = value.shape[0]
    sizes = [lax.axis_size(axis) for axis, _ in phases]
    scratch = [pltpu.VMEM((n, rows - first, LANES), F32) for n, (_, first) in zip(sizes, phases)]
    scratch += [pltpu.SemaphoreType.DMA((max(n - 1, 1),)) for n in sizes] * 2
    return pl.pallas_call(
        functools.partial(sum_kernel, phases),
        out_shape=jax.ShapeDtypeStruct(value.shape, F32),
        in_specs=[pl.BlockSpec(memory_space=pltpu.VMEM)],
        out_specs=pl.BlockSpec(memory_space=pltpu.VMEM),
        scratch_shapes=scratch,
        compiler_params=pltpu.CompilerParams(collective_id=ident, has_side_effects=True),
        name="small_sum",
    )(value)


def rows_of_lanes(flat, unit=8 * LANES):
    short = -flat.shape[0] % unit
    return jnp.pad(flat, (0, short)).reshape(-1, LANES)


def shifted(value, by):
    peers = lax.axis_size("seq")
    pairs = [(i, i + by) for i in range(peers) if 0 <= i + by < peers]
    return lax.ppermute(value, "seq", pairs)


def pad_last(value, to):
    short = to - value.shape[-1]
    if short == 0:
        return value
    return jnp.pad(value, [(0, 0)] * (value.ndim - 1) + [(0, short)])


def token_spec(width, col=0, flip=None):
    if flip is None:
        return pl.BlockSpec((1, L, width), lambda n, j: (n, j, col))
    return pl.BlockSpec((1, L, width), lambda n, j: (n, flip - 1 - j, col))


def span_spec(shape):
    return pl.BlockSpec((1,) + shape, lambda n, j: (n,) + (0,) * len(shape))


def whole_spec(shape):
    return pl.BlockSpec(shape, lambda n, j: (0,) * len(shape))


def shards(
    block_input,
    gain_in,
    w_zx,
    w_bc,
    w_dt,
    conv_x,
    conv_x_b,
    conv_bc,
    conv_bc_b,
    dt_bias,
    a_log,
    d_skip,
    gain_norm,
    w_out,
    cotangent,
):
    rows_dev, batch, model = block_input.shape
    tensor_count = lax.axis_size("tensor")
    span = rows_dev * tensor_count
    groups = span // L
    heads = dt_bias.shape[0]
    inner = gain_norm.shape[0]
    inner_total = inner * tensor_count
    state_n = conv_bc.shape[2]
    pairs = (heads + 1) // 2
    width = pairs * LANES
    tails = width + 3 * LANES
    wide = width + tails
    rows_w = w_out.shape[0]
    pspace = ("dp", "seq")

    mine_in = jnp.concatenate(
        [
            pad_last(w_zx[:, 0], width),
            pad_last(w_zx[:, 1], width),
            w_bc.reshape(rows_w, 2 * state_n),
            pad_last(w_dt, LANES),
        ],
        axis=1,
    )
    mine_o = pad_last(w_out, width)
    full_in = lax.all_gather(mine_in, pspace, axis=0, tiled=True)
    full_in, mine_o = lax.optimization_barrier((full_in, mine_o))
    full_o = lax.all_gather(mine_o, pspace, axis=0, tiled=True)

    flat_in = jnp.swapaxes(block_input, 0, 1).astype(F32)
    cot_rows = jnp.swapaxes(cotangent, 0, 1)
    inv_in = lax.rsqrt(jnp.mean(flat_in * flat_in, -1, keepdims=True) + EPS)
    base = flat_in * inv_in
    normed_rows = (base * gain_in).astype(BF)
    normed, cots = gather_tokens(normed_rows, cot_rows)
    halo_rows = shifted(normed[:, span - 8 :], 1)

    taps_x = pad_last(jnp.concatenate([conv_x, conv_x_b[None], jnp.zeros((3, inner), F32)], 0), width)
    taps_bc = jnp.concatenate(
        [
            conv_bc.reshape(4, 2 * state_n),
            conv_bc_b.reshape(1, 2 * state_n),
            jnp.zeros((3, 2 * state_n), F32),
        ],
        0,
    )
    small = pad_last(jnp.stack([dt_bias, -jnp.exp(a_log)] + [jnp.zeros_like(a_log)] * 6), LANES)
    chan = pad_last(
        jnp.stack([jnp.repeat(d_skip, HD), gain_norm] + [jnp.zeros_like(gain_norm)] * 6), width
    )

    pre = jnp.einsum("btd,dk->btk", normed, full_in, preferred_element_type=F32)
    halo = jnp.einsum("btd,dk->btk", halo_rows, full_in[:, width:], preferred_element_type=F32)
    grad_hidden = jnp.einsum("btd,dk->btk", cots, full_o, preferred_element_type=F32)

    params = pltpu.CompilerParams(
        dimension_semantics=("arbitrary", "arbitrary"), vmem_limit_bytes=VMEM_LIMIT
    )
    grid = (batch, groups)
    at_bc, at_dt = pairs, 2 * pairs + 2
    sds = jax.ShapeDtypeStruct
    x_act, ds_x, bc_act, ds_bc, step, cum, local_state, tot = pl.pallas_call(
        functools.partial(acts_kernel, pairs),
        grid=grid,
        out_shape=[
            sds((batch, span, width), F32),
            sds((batch, span, width), BF),
            sds((batch, span, 2 * LANES), F32),
            sds((batch, span, 2 * LANES), BF),
            sds((batch, span, LANES), F32),
            sds((batch, span, LANES), F32),
            sds((batch, LANES, width), F32),
            sds((batch, 8, LANES), F32),
        ],
        in_specs=[
            token_spec(width, 1),
            token_spec(2 * LANES, at_bc),
            token_spec(LANES, at_dt),
            span_spec((8, tails)),
            whole_spec((8, width)),
            whole_spec((8, 2 * LANES)),
            whole_spec((8, LANES)),
        ],
        out_specs=[
            token_spec(width),
            token_spec(width),
            token_spec(2 * LANES),
            token_spec(2 * LANES),
            token_spec(LANES),
            token_spec(LANES),
            span_spec((LANES, width)),
            span_spec((8, LANES)),
        ],
        scratch_shapes=[pltpu.VMEM((L + 8, width), F32), pltpu.VMEM((L + 8, 2 * LANES), F32)],
        compiler_params=params,
        name="acts",
    )(pre, pre, pre, halo, taps_x, taps_bc, small)

    tot_wide = jnp.repeat(tot[:, :, : 2 * pairs], HD, axis=-1)
    state_in = chain(local_state, tot_wide, 1, 3)

    mixed, ent, aft, stats = pl.pallas_call(
        functools.partial(forward_kernel, pairs),
        grid=grid,
        out_shape=[
            sds((batch, span, width), F32),
            sds((batch, groups, LANES, width), BF),
            sds((batch, groups, LANES, width), F32),
            sds((batch, 2, span), F32),
        ],
        in_specs=[
            token_spec(width),
            token_spec(2 * LANES),
            token_spec(LANES),
            token_spec(LANES),
            token_spec(width),
            token_spec(width),
            span_spec((LANES, width)),
            whole_spec((8, width)),
        ],
        out_specs=[
            token_spec(width),
            pl.BlockSpec((1, 1, LANES, width), lambda n, j: (n, j, 0, 0)),
            pl.BlockSpec((1, 1, LANES, width), lambda n, j: (n, j, 0, 0)),
            pl.BlockSpec((1, 2, L), lambda n, j: (n, 0, j)),
        ],
        scratch_shapes=[pltpu.VMEM((LANES, width), F32)],
        compiler_params=params,
        name="ssd_forward",
    )(x_act, bc_act, step, cum, pre, grad_hidden, state_in, chan)

    stats = small_sum(stats.reshape(-1, LANES), (("tensor", 0),), 4).reshape(stats.shape)

    grad_mixed, cot_gate, hidden, ds_local, sums_n = pl.pallas_call(
        functools.partial(gating_kernel, pairs, inner_total),
        grid=grid,
        out_shape=[
            sds((batch, span, width), F32),
            sds((batch, span, width), BF),
            sds((batch, span, width), BF),
            sds((batch, LANES, width), F32),
            sds((8, width), F32),
        ],
        in_specs=[
            token_spec(width),
            token_spec(2 * LANES),
            token_spec(LANES),
            token_spec(width),
            token_spec(width),
            token_spec(width),
            pl.BlockSpec((1, 2, L), lambda n, j: (n, 0, j)),
            whole_spec((8, width)),
        ],
        out_specs=[
            token_spec(width),
            token_spec(width),
            token_spec(width),
            span_spec((LANES, width)),
            whole_spec((8, width)),
        ],
        scratch_shapes=[pltpu.VMEM((8, LANES), F32)],
        compiler_params=params,
        name="gating_backward",
    )(x_act, bc_act, cum, pre, grad_hidden, mixed, stats, chan)

    carried = chain(ds_local, tot_wide, -1, 5)

    grad_o = jnp.einsum("btd,btk->dk", cots, hidden, preferred_element_type=F32).astype(BF)
    grad_z = jnp.einsum("btd,btk->dk", normed, cot_gate, preferred_element_type=F32).astype(BF)
    grad_oz = jnp.concatenate([grad_o, grad_z], axis=1)
    carried, grad_oz = lax.optimization_barrier((carried, grad_oz))
    red_oz = lax.psum_scatter(grad_oz, pspace, scatter_dimension=0, tiled=True)
    branch_part = jnp.einsum("btk,dk->btd", hidden, full_o, preferred_element_type=F32).astype(BF)
    branch = scatter_tokens(branch_part, 1)
    block_output = jnp.swapaxes((flat_in + branch).astype(BF), 0, 1)

    cot_in, tail, sums_x, sums_bc, sums_dt = pl.pallas_call(
        functools.partial(backward_kernel, pairs),
        grid=grid,
        out_shape=[
            sds((batch, span, wide), BF),
            sds((batch, 8, tails), F32),
            sds((8, width), F32),
            sds((8, 2 * LANES), F32),
            sds((8, LANES), F32),
        ],
        in_specs=[
            token_spec(width, 0, groups),
            token_spec(width, 0, groups),
            token_spec(width, 0, groups),
            token_spec(width, 0, groups),
            token_spec(2 * LANES, 0, groups),
            token_spec(2 * LANES, 0, groups),
            token_spec(LANES, 0, groups),
            token_spec(LANES, 0, groups),
            pl.BlockSpec((1, 1, LANES, width), lambda n, j: (n, groups - 1 - j, 0, 0)),
            pl.BlockSpec((1, 1, LANES, width), lambda n, j: (n, groups - 1 - j, 0, 0)),
            token_spec(width, 0, groups),
            token_spec(width, 1, groups),
            token_spec(2 * LANES, at_bc, groups),
            token_spec(LANES, at_dt, groups),
            span_spec((8, tails)),
            span_spec((LANES, width)),
            whole_spec((8, width)),
            whole_spec((8, width)),
            whole_spec((8, 2 * LANES)),
            whole_spec((8, LANES)),
        ],
        out_specs=[
            token_spec(wide, 0, groups),
            span_spec((8, tails)),
            whole_spec((8, width)),
            whole_spec((8, 2 * LANES)),
            whole_spec((8, LANES)),
        ],
        scratch_shapes=[
            pltpu.VMEM((LANES, width), F32),
            pltpu.VMEM((L + 8, width), F32),
            pltpu.VMEM((L + 8, 2 * LANES), F32),
        ],
        compiler_params=params,
        name="ssd_backward",
    )(
        grad_mixed,
        cot_gate,
        x_act,
        ds_x,
        bc_act,
        ds_bc,
        step,
        cum,
        ent,
        aft,
        mixed,
        pre,
        pre,
        pre,
        halo,
        carried,
        chan,
        taps_x,
        taps_bc,
        small,
    )
    later = shifted(tail, -1)
    cot_in = cot_in.at[:, span - 8 :, width:].add(later.astype(BF))

    grad_wx = jnp.einsum("btd,btk->dk", normed, cot_in[..., width:], preferred_element_type=F32)
    grad_wx, cot_in = lax.optimization_barrier((grad_wx.astype(BF), cot_in))
    red_x = lax.psum_scatter(grad_wx, pspace, scatter_dimension=0, tiled=True)
    part = jnp.einsum("btk,dk->btd", cot_in, full_in, preferred_element_type=F32).astype(BF)
    grad_normed = scatter_tokens(part, 2)

    scaled = grad_normed * gain_in
    grad_base = inv_in * (scaled - base * jnp.mean(scaled * base, -1, keepdims=True))
    input_grad = jnp.swapaxes((cot_rows.astype(F32) + grad_base).astype(BF), 0, 1)
    gain_part = jnp.sum(grad_normed * base, (0, 1))

    sizes_own = (
        sums_x[:5, :inner].reshape(-1),
        sums_n[0, :inner],
        jnp.sum(sums_n[1, :inner].reshape(heads, HD), -1),
        sums_dt[0, :heads],
        sums_dt[1, :heads],
    )
    mine = rows_of_lanes(jnp.concatenate(sizes_own))
    rest = rows_of_lanes(jnp.concatenate([sums_bc[:5].reshape(-1), gain_part]))
    first = mine.shape[0]
    summed = small_sum(
        jnp.concatenate([mine, rest], 0), (("dp", 0), ("seq", 0), ("tensor", first)), 6
    )
    own, shared = summed[:first].reshape(-1), summed[first:].reshape(-1)
    part_bc = red_x[:, width : width + 2 * state_n].astype(F32)
    grad_bc = small_sum(part_bc.reshape(-1, LANES), (("tensor", 0),), 7)

    n5 = 5 * inner
    bc5 = 5 * 2 * state_n
    return (
        block_output,
        input_grad,
        shared[bc5 : bc5 + model],
        jnp.stack([red_oz[:, width : width + inner], red_x[:, :inner]], 1).astype(F32),
        grad_bc.reshape(rows_w, 2, state_n),
        red_x[:, width + 2 * state_n : width + 2 * state_n + heads].astype(F32),
        own[: 4 * inner].reshape(4, inner),
        own[4 * inner : n5],
        shared[: 4 * 2 * state_n].reshape(4, 2, state_n),
        shared[4 * 2 * state_n : bc5].reshape(2, state_n),
        own[n5 + inner + heads : n5 + inner + 2 * heads],
        own[n5 + inner + 2 * heads : n5 + inner + 3 * heads],
        own[n5 + inner : n5 + inner + heads],
        own[n5 : n5 + inner],
        red_oz[:, :inner].astype(F32),
    )


def solution(mesh):
    return jax.shard_map(
        shards,
        mesh=mesh,
        in_specs=(
            P(("seq", "tensor"), "dp", None),
            P(),
            P(("dp", "seq"), None, "tensor"),
            P(("dp", "seq"), None, None),
            P(("dp", "seq"), "tensor"),
            P(None, "tensor"),
            P("tensor"),
            P(),
            P(),
            P("tensor"),
            P("tensor"),
            P("tensor"),
            P("tensor"),
            P(("dp", "seq"), "tensor"),
            P(("seq", "tensor"), "dp", None),
        ),
        out_specs=(
            P(("seq", "tensor"), "dp", None),
            P(("seq", "tensor"), "dp", None),
            P(),
            P(("dp", "seq"), None, "tensor"),
            P(("dp", "seq"), None, None),
            P(("dp", "seq"), "tensor"),
            P(None, "tensor"),
            P("tensor"),
            P(),
            P(),
            P("tensor"),
            P("tensor"),
            P("tensor"),
            P("tensor"),
            P(("dp", "seq"), "tensor"),
        ),
        check_vma=False,
    )
```

time: 1420 us -> 541 us (0.38)
  waiting for transfers between devices: 565 us -> 33.3 us
  Pallas kernels: 0 us -> 330 us
  matrix products: 292 us -> 87.3 us
  local copies, waits for them, and re-layouts: 202 us -> 45.2 us
  other arithmetic: 170 us -> 15.6 us
  blocking collectives: 139 us -> 0 us
    pallas_call x0 -> x12, Pallas kernels: none -> 330 us  [the longest x2 77.4 us: scatter_tokens(): pl.pallas_call(functools.partial(scatter_kernel, cuts), out_shape=jax.Sha...]
    reduce_scatter x6 -> x1, waiting for transfers between devices: 287 us -> 0.01 us  [shards(): red_x = lax.psum_scatter(grad_wx, pspace, scatter_dimension=0, tiled=True)]
    dot_general x52 -> x8, matrix products: 292 us -> 87.3 us  [the longest x1 18.4 us: shards(): pre = jnp.einsum('btd,dk->btk', normed, full_in, preferred_element_type=F32)]
    psum x2 -> x0, waiting for transfers between devices: 168 us -> none  [the longest x1 124 us: shards(): lax.psum((spread_out(small_acc[0], tensor_rank, 1, tensor_count), spread_...]
    all_gather x4 -> x0, blocking collectives: 107 us -> none  [the longest x2 37.8 us: entering_2(): lax.all_gather(part.astype(kind), axis)]
    reduce_sum x21 -> x3, other arithmetic: 56.4 us -> 1.47 us  [the longest x1 0.97 us: shards(): gain_part = jnp.sum(grad_normed * base, (0, 1))]
    reshape x18 -> x9, local copies, waits for them, and re-layouts: 56.2 us -> 4.7 us  [the longest x1 1.34 us: shards(): stats.reshape(-1, LANES)]
    unnamed x20 -> x5, waiting for transfers between devices: 68.9 us -> 19.2 us
  transfers between devices with their start and end apart: 26 -> 6, of which waited for: 13 -> 3; matrix products, arithmetic and copies ran while one was open for 26% -> 15% of each run, Pallas kernels for 0% -> 40%
where the time goes in v1:
time: 541 us; the launch traced here: 532 us
  Pallas kernels  330 us (61%)
  matrix products  87.3 us (16%)
  local copies, waits for them, and re-layouts  45.2 us (8%)
  waiting for transfers between devices  33.3 us (6%)
  other arithmetic  15.6 us (3%)
  between operations  14.6 us (3%)
    pallas_call x2, Pallas kernels, scatter_tokens(): pl.pallas_call(functools.partial(scatter_kernel, cuts), out_shape=jax.Sha...  77.4 us
    pallas_call x1, Pallas kernels, gather_tokens(): pl.pallas_call(functools.partial(gather_kernel, cuts, count), out_shape=[...  73.7 us
    pallas_call x2, Pallas kernels, chain(): pl.pallas_call(functools.partial(chain_kernel, by, cuts), out_shape=jax.S...  43.9 us
    pallas_call x1, Pallas kernels, shards(): pl.pallas_call(functools.partial(backward_kernel, pairs), grid=grid, out_...  42.6 us
    pallas_call x3, Pallas kernels, small_sum(): pl.pallas_call(functools.partial(sum_kernel, phases), out_shape=jax.Shape...  31 us
    unnamed x66, local copies, waits for them, and re-layouts  26.4 us
    pallas_call x1, Pallas kernels, shards(): pl.pallas_call(functools.partial(forward_kernel, pairs), grid=grid, out_s...  24.5 us
    unnamed x5, waiting for transfers between devices  19.2 us
  transfers between devices with their start and end apart: 6, of which 3 were waited for; matrix products, arithmetic and copies ran while one was open for 15% of the time, Pallas kernels for 40%

profile of v1, /device:TPU:0, one launch (start us, length us, event | category | flops | bytes accessed | tf_op | source)
XLA Modules:
  0.0 531.6 jit_solution(3564835529351974334)
XLA Ops:
  9.0 2.6 fusion.34
  14.2 73.7 %gather_tokens.1 = (bf16[2,1024,1536]{2,1,0:T(8,128)(2,1)S(1)}, bf16[2,1024,1536]{2,1,0:T(8,128)(2,1)S(1)}) custom-call(bf16[2,256,1536]{2,1,0:T(8,128)(2,1)S(1)} %fusion.16.refs_0_, bf16[2,256,1536]{2,1,0:T(8,128)(2,1)S(1)} %bitcast.117), custom_call_target="tpu_custom_call" | custom-call | tf_op jit(solution)/shard_map/gather_tokens/pallas_call | solution.py:557
  87.8 2.6 copy-done.3
  90.5 2.7 copy-done.1
  93.2 3.5 collective-permute-start
  99.8 9.5 %all-gather.3.cloned.1.call-done = bf16[1536,1920]{1,0:T(8,128)(2,1)} async-done(((bf16[192,1920]{1,0:T(8,128)(2,1)}), bf16[1536,1920]{1,0:T(8,128)(2,1)}) %all-gather.3.cloned.1.call-update) | async-done | bytes 5898256 | tf_op jit(solution)/shard_map/all_gather | solution.py:859
  109.4 3.4 fusion.9.halo_ref
  113.3 18.4 %fusion.3.x_ref.bc_ref.dt_ref.gate_ref.px_ref.pbc_ref.pdt_ref = f32[2,1024,1920]{2,1,0:T(8,128)} fusion(bf16[2,1024,1536]{2,1,0:T(8,128)(2,1)S(1)} %copy-done.2, bf16[1536,1920]{1,0:T(8,128)(2,1)} %all-gather.3.cloned.1.call-done), kind=kOutput, calls=%fused_computation.4 | convolution fusion | flops 12079595520 | bytes 27918336 | tf_op jit(solution)/shard_map/btd,dk->btk/dot_general | solution.py:885
  131.7 18.9 %acts.1 = (f32[2,1024,768]{2,1,0:T(8,128)}, bf16[2,1024,768]{2,1,0:T(8,128)(2,1)}, f32[2,1024,256]{2,1,0:T(8,128)}, bf16[2,1024,256]{2,1,0:T(8,128)(2,1)}, f32[2...) custom-call(f32[2,1024,1920]{2,1,0:T(8,128)} %fusion.3.x_ref.bc_ref.dt_ref.gate_ref, ...), custom_call_target="tpu_custom_call" | custom-call | tf_op jit(solution)/shard_map/acts/pallas_call | solution.py:895
  152.1 16.8 %chain.2.in_ref = f32[2,128,768]{2,1,0:T(8,128)} custom-call(f32[2,128,768]{2,1,0:T(8,128)} %get-tuple-element.65.own_ref, f32[2,8,768]{2,1,0:T(8,128)} %reshape.142.tot_ref), custom_call_target="tpu_custom_call" | custom-call | tf_op jit(solution)/shard_map/chain/pallas_call | solution.py:715
  168.9 9.6 %fusion.26.gh_ref = f32[2,1024,768]{2,1,0:T(8,128)} fusion(bf16[2,1024,1536]{2,1,0:T(8,128)(2,1)} %copy-done.3, bf16[1536,768]{1,0:T(8,128)(2,1)} %all-gather.5.cloned.1.call-done), kind=kOutput, calls=%fused_computation.32 | convolution fusion | flops 4831838208 | bytes 14942208 | tf_op jit(solution)/shard_map/btd,dk->btk/dot_general | solution.py:887
  178.5 24.5 %ssd_forward.1 = (f32[2,1024,768]{2,1,0:T(8,128)}, bf16[2,4,128,768]{3,2,1,0:T(8,128)(2,1)}, f32[2,4,128,768]{3,2,1,0:T(8,128)}, f32[2,2,1024]{2,1,0:T(2,128)}) custom-call(f32[2,1024,768]{2,1,0:T(8,128)} %get-tuple-element.59.x_ref, f32[2,1024,256]{2,1,0:T(8,128)} %get-tuple-element.60.bc_ref, f32[2,1024,128]{2,1,0:T(8,128)} %get-tuple-element.64.time_ref, ...), custom_call_target="tpu_custom_call" | custom-call | tf_op jit(solution)/shard_map/ssd_forward/pallas_call | solution.py:935
  204.2 5.1 small_sum.3
  210.7 18.5 %gating_backward.1 = (f32[2,1024,768]{2,1,0:T(8,128)}, bf16[2,1024,768]{2,1,0:T(8,128)(2,1)}, bf16[2,1024,768]{2,1,0:T(8,128)(2,1)}, f32[2,128,768]{2,1,0:T(8,128)}, f32[8,768]{1,0:T(8,128)}) custom-call(f32[2,1024,768]{2,1,0:T(8,128)} %get-tuple-element.59.x_ref, f32[2,1024,256]{2,1,0:T(8,128)} %get-tuple-element.60.bc_ref, ...), custom_call_target="tpu_custom_call" | custom-call | tf_op jit(solution)/shard_map/gating_backward/pallas_call | solution.py:967
  229.2 9.7 %bitcast_convert_fusion.1 = bf16[1536,768]{0,1:T(8,128)(2,1)} fusion(bf16[2,1024,1536]{2,1,0:T(8,128)(2,1)} %copy-done.3, bf16[2,1024,768]{2,1,0:T(8,128)(2,1)} %get-tuple-element.69), kind=kOutput, calls=%fused_computation.11 | convolution fusion | flops 4833017856 | bytes 11796480 | tf_op jit(solution)/shard_map/btd,btk->dk/dot_general | solution.py:1001
  239.0 27.1 %chain.3.carried_ref = f32[2,128,768]{2,1,0:T(8,128)} custom-call(f32[2,128,768]{2,1,0:T(8,128)} %get-tuple-element.76.own_ref, f32[2,8,768]{2,1,0:T(8,128)} %reshape.142.tot_ref), custom_call_target="tpu_custom_call" | custom-call | tf_op jit(solution)/shard_map/chain/pallas_call | solution.py:715
  266.1 8.3 %bitcast_convert_fusion = bf16[1536,768]{0,1:T(8,128)(2,1)S(1)} fusion(bf16[2,1024,1536]{2,1,0:T(8,128)(2,1)} %copy-done.1, bf16[2,1024,768]{2,1,0:T(8,128)(2,1)S(1)} %copy-done.7), kind=kOutput, calls=%fused_computation.10 | convolution fusion | flops 4833017856 | bytes 11796480 | tf_op jit(solution)/shard_map/btd,btk->dk/dot_general | solution.py:1002
  274.4 2.4 pad_maximum_fusion
  276.8 42.6 %ssd_backward.1 = (bf16[2,1024,1920]{2,1,0:T(8,128)(2,1)}, f32[2,8,1152]{2,1,0:T(8,128)}, f32[8,768]{1,0:T(8,128)}, f32[8,256]{1,0:T(8,128)}, f32[8,128]{1,0:T(8,128)}) custom-call(f32[2,1024,768]{2,1,0:T(8,128)} %get-tuple-element.70.grad_ref, bf16[2,1024,768]{2,1,0:T(8,128)(2,1)} %get-tuple-element.71.cgate_ref, f32[2,1024,768]{2,1,0:T(8,128)} %get-tuple-element.59.x_ref, ...), custom_call_target="tpu_custom_call" | custom-call | tf_op jit(solution)/shard_map/ssd_backward/pallas_call | solution.py:1010
  321.7 4.6 collective-permute-done.1
  327.6 13.2 %fusion = bf16[1536,1152]{1,0:T(8,128)(2,1)} fusion(bf16[2,1024,1536]{2,1,0:T(8,128)(2,1)} %copy-done.1, bf16[2,1024,1920]{2,1,0:T(8,128)(2,1)} %add_dynamic-update-slice_fusion), kind=kOutput, calls=%fused_computation.1 | convolution fusion | flops 7249526784 | bytes 14548992 | tf_op jit(solution)/shard_map/btd,btk->dk/dot_general | solution.py:1081
  341.0 6.7 %copy.89 = bf16[1536,1536]{1,0:T(8,128)(2,1)} copy(bf16[1536,1536]{0,1:T(8,128)(2,1)} %pad_maximum_fusion) | data formatting | bytes 9437184
  349.4 7.2 %convolution_convert_fusion.in_ref = bf16[2,1024,1536]{2,1,0:T(8,128)(2,1)S(1)} fusion(bf16[2,1024,768]{2,1,0:T(8,128)(2,1)} %get-tuple-element.69, bf16[1536,768]{1,0:T(8,128)(2,1)S(1)} %copy-done.24), kind=kOutput, calls=%fused_computation.6 | convolution fusion | flops 4834983936 | bytes 11796480 | tf_op jit(solution)/shard_map/btk,dk->btd/dot_general | solution.py:1006
  356.7 38.8 %scatter_tokens.2 = f32[2,256,1536]{2,1,0:T(8,128)S(1)} custom-call(bf16[2,1024,1536]{2,1,0:T(8,128)(2,1)S(1)} %convolution_convert_fusion.in_ref), custom_call_target="tpu_custom_call" | custom-call | tf_op jit(solution)/shard_map/scatter_tokens/pallas_call | solution.py:637
  398.0 17.6 %fusion.5.in_ref = bf16[2,1024,1536]{2,1,0:T(8,128)(2,1)S(1)} fusion(bf16[2,1024,1920]{2,1,0:T(8,128)(2,1)} %add_dynamic-update-slice_fusion, bf16[1536,1920]{1,0:T(8,128)(2,1)} %all-gather.3.cloned.1.call-done), kind=kOutput, calls=%fused_computation.7 | convolution fusion | flops 12082741248 | bytes 20054016 | tf_op jit(solution)/shard_map/btk,dk->btd/dot_general | solution.py:1084
  415.7 38.6 %scatter_tokens.3 = f32[2,256,1536]{2,1,0:T(8,128)S(1)} custom-call(bf16[2,1024,1536]{2,1,0:T(8,128)(2,1)S(1)} %fusion.5.in_ref), custom_call_target="tpu_custom_call" | custom-call | tf_op jit(solution)/shard_map/scatter_tokens/pallas_call | solution.py:637
  455.9 13.9 %small_sum.4 = f32[64,128]{1,0:T(8,128)} custom-call(f32[64,128]{1,0:T(8,128)} %pad_maximum_fusion.1.in_ref), custom_call_target="tpu_custom_call" | custom-call | tf_op jit(solution)/shard_map/small_sum/pallas_call | solution.py:774
  473.6 3.6 fusion.29
  477.2 2.8 copy.83
  480.0 2.8 copy.82
  487.7 12.0 %small_sum.5 = f32[384,128]{1,0:T(8,128)} custom-call(f32[384,128]{1,0:T(8,128)} %reshape.156.in_ref), custom_call_target="tpu_custom_call" | custom-call | tf_op jit(solution)/shard_map/small_sum/pallas_call | solution.py:774
  500.9 19.2 %reduce-scatter.7.cloned.1.call-done = bf16[192,1536]{1,0:T(8,128)(2,1)} async-done(((bf16[1536,1536]{1,0:T(8,128)(2,1)}), bf16[192,1536]{1,0:T(8,128)(2,1)}) %reduce-scatter.7.cloned.1.call-update) | async-done | bytes 589840
  (128 shorter events, 36.4 us)
Async XLA Ops:
  7.2 102.2 %all-gather.3.cloned.1.call-start = ((), (), s32[]{:S(2)}) async-start(), calls=%async_computation.2 | async-start | bytes 6635520 | tf_op jit(solution)/shard_map/all_gather | solution.py:859
  9.0 3.7 copy-start.6
  11.5 1.7 copy-start.4
  11.6 2.0 copy-start.11
  12.6 156.3 %all-gather.5.cloned.1.call-start = ((), (), s32[]{:S(2)}) async-start(), calls=%async_computation.3 | async-start | bytes 2654208 | tf_op jit(solution)/shard_map/all_gather | solution.py:861
  13.6 74.2 %copy-start.13 = (f32[2,256]{1,0:T(2,128)}, f32[2,256]{1,0:T(2,128)S(1)}, u32[]{:S(2)}) copy-start(f32[2,256]{1,0:T(2,128)S(1)} %add_rsqrt_fusion) | copy-start | bytes 6148
  13.6 83.3 %copy-start.18 = (f32[768]{0:T(1024)S(1)}, f32[768]{0:T(1024)}, u32[]{:S(2)}) copy-start(f32[768]{0:T(1024)} %param.23) | copy-start | bytes 9220
  13.6 83.3 %copy-start.19 = (f32[768]{0:T(1024)S(1)}, f32[768]{0:T(1024)}, u32[]{:S(2)}) copy-start(f32[768]{0:T(1024)} %param.29) | copy-start | bytes 9220
  13.6 83.3 %copy-start.20 = (f32[4,2,128]{2,1,0:T(2,128)S(1)}, f32[4,2,128]{2,1,0:T(2,128)}, u32[]{:S(2)}) copy-start(f32[4,2,128]{2,1,0:T(2,128)} %param.24) | copy-start | bytes 12292
  13.7 83.3 %copy-start.22 = (f32[12]{0:T(128)S(1)}, f32[12]{0:T(128)}, u32[]{:S(2)}) copy-start(f32[12]{0:T(128)} %param.28) | copy-start | bytes 148
  13.7 83.4 %copy-start.25 = (f32[12]{0:T(128)S(1)}, f32[12]{0:T(128)}, u32[]{:S(2)}) copy-start(f32[12]{0:T(128)} %param.27) | copy-start | bytes 148
  13.7 83.4 %copy-start.21 = (f32[2,128]{1,0:T(2,128)S(1)}, f32[2,128]{1,0:T(2,128)}, u32[]{:S(2)}) copy-start(f32[2,128]{1,0:T(2,128)} %param.25) | copy-start | bytes 3076
  13.7 84.1 %copy-start.16 = (f32[4,768]{1,0:T(4,128)S(1)}, f32[4,768]{1,0:T(4,128)}, u32[]{:S(2)}) copy-start(f32[4,768]{1,0:T(4,128)} %param.22) | copy-start | bytes 36868
  13.7 85.4 %copy-start.23 = (f32[12]{0:T(128)S(1)}, f32[12]{0:T(128)}, u32[]{:S(2)}) copy-start(f32[12]{0:T(128)} %param.26) | copy-start | bytes 148
  87.8 2.6 copy-start.3
  90.5 2.7 copy-start.1
  93.2 16.3 %collective-permute-start = (bf16[2,8,1536]{2,1,0:T(8,128)(2,1)S(1)}, bf16[2,8,1536]{2,1,0:T(8,128)(2,1)S(1)}, u32[]{:S(2)}, u32[]{:S(2)}) collective-permute-start(bf16[2,8,1536]{2,1,0:T(8,128)(2,1)S(1)} %slice.132), channel_id=1, source_target_pairs={{0,4},{4,8},{8,12},{1,5},{5,9},{9,13},{2,6},{6,10},{10,14},{3,7},{... | collective-permute-start | bytes 147464 | tf_op jit(solution)/shard_map/ppermute | solution.py:793
  109.4 375.2 %reduce-scatter.9.cloned.1.call-start = ((), (), s32[]{:S(2)}) async-start(), calls=%async_computation.5 | async-start | bytes 3981312 | tf_op jit(solution)/shard_map/reduce_scatter | solution.py:1083
  109.4 3.9 copy-start.2
  229.2 36.9 %copy-start.7 = (bf16[2,1024,768]{2,1,0:T(8,128)(2,1)S(1)}, bf16[2,1024,768]{2,1,0:T(8,128)(2,1)}, u32[]{:S(2)}) copy-start(bf16[2,1024,768]{2,1,0:T(8,128)(2,1)} %get-tuple-element.71.cgate_ref) | copy-start | bytes 9437188
  266.1 8.3 %copy-start.8 = (bf16[1536,768]{0,1:T(8,128)(2,1)S(1)}, bf16[1536,768]{0,1:T(8,128)(2,1)}, u32[]{:S(2)}) copy-start(bf16[1536,768]{0,1:T(8,128)(2,1)} %bitcast_convert_fusion.1) | copy-start | bytes 7077892
  320.4 5.8 %collective-permute-start.1 = (bf16[2,8,1152]{2,1,0:T(8,128)(2,1)S(1)}, bf16[2,8,1152]{2,1,0:T(8,128)(2,1)S(1)}, u32[]{:S(2)}, u32[]{:S(2)}) collective-permute-start(bf16[2,8,1152]{2,1,0:T(8,128)(2,1)S(1)} %convert.2), channel_id=1, source_target_pairs={{4,0},{8,4},{12,8},{5,1},{9,5},{13,9},{6,2},{10,6},{14,10},{7,3},{... | collective-permute-start | bytes 110600 | tf_op jit(solution)/shard_map/ppermute | solution.py:793
  340.8 179.2 %reduce-scatter.7.cloned.1.call-start = ((), (), s32[]{:S(2)}) async-start(), calls=%async_computation.4 | async-start | bytes 5308416
  347.7 1.2 copy-start.17
  347.7 1.2 copy-start.15
  347.7 1.7 copy-start.24
  395.5 1.7 copy-start
  415.6 38.6 %copy-start.5 = (bf16[256,2,1536]{2,1,0:T(2,128)(2,1)S(1)}, bf16[256,2,1536]{2,1,0:T(2,128)(2,1)}, u32[]{:S(2)}) copy-start(bf16[256,2,1536]{2,1,0:T(2,128)(2,1)} %param.17) | copy-start | bytes 4718596
  415.6 38.6 %copy-start.12 = (f32[1536]{0:T(1024)S(1)}, f32[1536]{0:T(1024)}, u32[]{:S(2)}) copy-start(f32[1536]{0:T(1024)} %param.18) | copy-start | bytes 18436
  415.7 38.6 %copy-start.14 = (f32[2,256]{1,0:T(2,128)S(1)}, f32[2,256]{1,0:T(2,128)}, u32[]{:S(2)}) copy-start(f32[2,256]{1,0:T(2,128)} %copy-done.13) | copy-start | bytes 6148
  477.2 5.5 %copy-start.10 = (f32[64,128]{1,0:T(8,128)S(1)}, f32[64,128]{1,0:T(8,128)}, u32[]{:S(2)}) copy-start(f32[64,128]{1,0:T(8,128)} %small_sum.4) | copy-start | bytes 98308
  522.3 1.8 copy-start.9
Sparse Core Ops, SparseCore 0:
  12.7 96.6 all-gather.2
  111.4 54.4 all-gather.4
  340.9 76.6 reduce-scatter.8
  421.1 98.8 reduce-scatter.6

commit v2 on v1

--- a/solution.py
+++ b/solution.py
@@ -4,6 +4,7 @@
 import jax.numpy as jnp
 from jax import lax
 from jax.experimental import pallas as pl
+from jax.experimental.layout import Layout, with_layout_constraint
 from jax.experimental.pallas import tpu as pltpu
 from jax.sharding import PartitionSpec as P
 
@@ -1000,12 +1001,13 @@
 
     grad_o = jnp.einsum("btd,btk->dk", cots, hidden, preferred_element_type=F32).astype(BF)
     grad_z = jnp.einsum("btd,btk->dk", normed, cot_gate, preferred_element_type=F32).astype(BF)
-    grad_oz = jnp.concatenate([grad_o, grad_z], axis=1)
+    grad_oz = with_layout_constraint(
+        jnp.concatenate([grad_o, grad_z], axis=1), Layout(major_to_minor=(0, 1))
+    )
     carried, grad_oz = lax.optimization_barrier((carried, grad_oz))
     red_oz = lax.psum_scatter(grad_oz, pspace, scatter_dimension=0, tiled=True)
     branch_part = jnp.einsum("btk,dk->btd", hidden, full_o, preferred_element_type=F32).astype(BF)
     branch = scatter_tokens(branch_part, 1)
-    block_output = jnp.swapaxes((flat_in + branch).astype(BF), 0, 1)
 
     cot_in, tail, sums_x, sums_bc, sums_dt = pl.pallas_call(
         functools.partial(backward_kernel, pairs),
@@ -1079,7 +1081,10 @@
     cot_in = cot_in.at[:, span - 8 :, width:].add(later.astype(BF))
 
     grad_wx = jnp.einsum("btd,btk->dk", normed, cot_in[..., width:], preferred_element_type=F32)
-    grad_wx, cot_in = lax.optimization_barrier((grad_wx.astype(BF), cot_in))
+    grad_wx, cot_in, red_oz, branch = lax.optimization_barrier(
+        (grad_wx.astype(BF), cot_in, red_oz, branch)
+    )
+    block_output = jnp.swapaxes((flat_in + branch).astype(BF), 0, 1)
     red_x = lax.psum_scatter(grad_wx, pspace, scatter_dimension=0, tiled=True)
     part = jnp.einsum("btk,dk->btd", cot_in, full_in, preferred_element_type=F32).astype(BF)
     grad_normed = scatter_tokens(part, 2)

time: 541 us -> 515 us (0.952)
  waiting for transfers between devices: 33.3 us -> 9.62 us
  starting transfers between devices: 5.08 us -> 15.6 us
  local copies, waits for them, and re-layouts: 45.2 us -> 34.9 us
    unnamed x5 -> x4, waiting for transfers between devices: 19.2 us -> 0.07 us
    reduce_scatter x1, starting transfers between devices: 0.04 us -> 10.7 us  [shards(): red_x = lax.psum_scatter(grad_wx, pspace, scatter_dimension=0, tiled=True)]
    unnamed x66 -> x65, local copies, waits for them, and re-layouts: 26.4 us -> 18.7 us
  transfers between devices with their start and end apart: 6 -> 6, of which waited for: 3 -> 1; matrix products, arithmetic and copies ran while one was open for 15% -> 17% of each run, Pallas kernels for 40% -> 48%
where the time goes in v2:
time: 515 us; the launch traced here: 510 us
  Pallas kernels  332 us (64%)
  matrix products  85.7 us (17%)
  local copies, waits for them, and re-layouts  34.9 us (7%)
  other arithmetic  17.3 us (3%)
  starting transfers between devices  15.6 us (3%)
  between operations  14.6 us (3%)
  waiting for transfers between devices  9.62 us (2%)
    pallas_call x2, Pallas kernels, scatter_tokens(): pl.pallas_call(functools.partial(scatter_kernel, cuts), out_shape=jax.Sha...  77.5 us
    pallas_call x1, Pallas kernels, gather_tokens(): pl.pallas_call(functools.partial(gather_kernel, cuts, count), out_shape=[...  73.7 us
    pallas_call x2, Pallas kernels, chain(): pl.pallas_call(functools.partial(chain_kernel, by, cuts), out_shape=jax.S...  43.6 us
    pallas_call x1, Pallas kernels, shards(): pl.pallas_call(functools.partial(backward_kernel, pairs), grid=grid, out_...  42.8 us
    pallas_call x3, Pallas kernels, small_sum(): pl.pallas_call(functools.partial(sum_kernel, phases), out_shape=jax.Shape...  32.6 us
    pallas_call x1, Pallas kernels, shards(): pl.pallas_call(functools.partial(forward_kernel, pairs), grid=grid, out_s...  24.5 us
    pallas_call x1, Pallas kernels, shards(): pl.pallas_call(functools.partial(acts_kernel, pairs), grid=grid, out_shap...  18.9 us
    unnamed x65, local copies, waits for them, and re-layouts  18.7 us
  transfers between devices with their start and end apart: 6, of which 1 were waited for; matrix products, arithmetic and copies ran while one was open for 17% of the time, Pallas kernels for 48%

profile of v2, /device:TPU:0, one launch (start us, length us, event | category | flops | bytes accessed | tf_op | source)
XLA Modules:
  0.0 509.8 jit_solution(7316134054834999594)
XLA Ops:
  9.0 2.6 fusion.33
  14.2 73.7 %gather_tokens.1 = (bf16[2,1024,1536]{2,1,0:T(8,128)(2,1)S(1)}, bf16[2,1024,1536]{2,1,0:T(8,128)(2,1)S(1)}) custom-call(bf16[2,256,1536]{2,1,0:T(8,128)(2,1)S(1)} %fusion.16.refs_0_, bf16[2,256,1536]{2,1,0:T(8,128)(2,1)S(1)} %bitcast.117), custom_call_target="tpu_custom_call" | custom-call | tf_op jit(solution)/shard_map/gather_tokens/pallas_call | solution.py:558
  87.8 2.6 copy-done.3
  90.5 2.7 copy-done.1
  93.2 3.5 collective-permute-start
  99.8 9.5 %all-gather.3.cloned.1.call-done = bf16[1536,1920]{1,0:T(8,128)(2,1)} async-done(((bf16[192,1920]{1,0:T(8,128)(2,1)}), bf16[1536,1920]{1,0:T(8,128)(2,1)}) %all-gather.3.cloned.1.call-update) | async-done | bytes 5898256 | tf_op jit(solution)/shard_map/all_gather | solution.py:860
  109.4 3.4 fusion.9.halo_ref
  113.3 18.4 %fusion.3.x_ref.bc_ref.dt_ref.gate_ref.px_ref.pbc_ref.pdt_ref = f32[2,1024,1920]{2,1,0:T(8,128)} fusion(bf16[2,1024,1536]{2,1,0:T(8,128)(2,1)S(1)} %copy-done.2, bf16[1536,1920]{1,0:T(8,128)(2,1)} %all-gather.3.cloned.1.call-done), kind=kOutput, calls=%fused_computation.4 | convolution fusion | flops 12079595520 | bytes 27918336 | tf_op jit(solution)/shard_map/btd,dk->btk/dot_general | solution.py:886
  131.7 18.9 %acts.1 = (f32[2,1024,768]{2,1,0:T(8,128)}, bf16[2,1024,768]{2,1,0:T(8,128)(2,1)}, f32[2,1024,256]{2,1,0:T(8,128)}, bf16[2,1024,256]{2,1,0:T(8,128)(2,1)}, f32[2...) custom-call(f32[2,1024,1920]{2,1,0:T(8,128)} %fusion.3.x_ref.bc_ref.dt_ref.gate_ref, ...), custom_call_target="tpu_custom_call" | custom-call | tf_op jit(solution)/shard_map/acts/pallas_call | solution.py:896
  152.1 16.8 %chain.2.in_ref = f32[2,128,768]{2,1,0:T(8,128)} custom-call(f32[2,128,768]{2,1,0:T(8,128)} %get-tuple-element.67.own_ref, f32[2,8,768]{2,1,0:T(8,128)} %reshape.142.tot_ref), custom_call_target="tpu_custom_call" | custom-call | tf_op jit(solution)/shard_map/chain/pallas_call | solution.py:716
  168.9 9.6 %fusion.26.gh_ref = f32[2,1024,768]{2,1,0:T(8,128)} fusion(bf16[2,1024,1536]{2,1,0:T(8,128)(2,1)} %copy-done.3, bf16[1536,768]{1,0:T(8,128)(2,1)} %all-gather.5.cloned.1.call-done), kind=kOutput, calls=%fused_computation.32 | convolution fusion | flops 4831838208 | bytes 14942208 | tf_op jit(solution)/shard_map/btd,dk->btk/dot_general | solution.py:888
  178.5 24.5 %ssd_forward.1 = (f32[2,1024,768]{2,1,0:T(8,128)}, bf16[2,4,128,768]{3,2,1,0:T(8,128)(2,1)}, f32[2,4,128,768]{3,2,1,0:T(8,128)}, f32[2,2,1024]{2,1,0:T(2,128)}) custom-call(f32[2,1024,768]{2,1,0:T(8,128)} %get-tuple-element.61.x_ref, f32[2,1024,256]{2,1,0:T(8,128)} %get-tuple-element.62.bc_ref, f32[2,1024,128]{2,1,0:T(8,128)} %get-tuple-element.66.time_ref, ...), custom_call_target="tpu_custom_call" | custom-call | tf_op jit(solution)/shard_map/ssd_forward/pallas_call | solution.py:936
  204.4 5.1 %small_sum.3 = f32[32,128]{1,0:T(8,128)} custom-call(f32[32,128]{1,0:T(8,128)} %reshape.143.in_ref), custom_call_target="tpu_custom_call" | custom-call | tf_op jit(solution)/shard_map/small_sum/pallas_call | solution.py:775
  210.9 18.6 %gating_backward.1 = (f32[2,1024,768]{2,1,0:T(8,128)}, bf16[2,1024,768]{2,1,0:T(8,128)(2,1)}, bf16[2,1024,768]{2,1,0:T(8,128)(2,1)}, f32[2,128,768]{2,1,0:T(8,128)}, f32[8,768]{1,0:T(8,128)}) custom-call(f32[2,1024,768]{2,1,0:T(8,128)} %get-tuple-element.61.x_ref, f32[2,1024,256]{2,1,0:T(8,128)} %get-tuple-element.62.bc_ref, ...), custom_call_target="tpu_custom_call" | custom-call | tf_op jit(solution)/shard_map/gating_backward/pallas_call | solution.py:968
  229.5 9.4 %bitcast_convert_fusion.1 = bf16[1536,768]{1,0:T(8,128)(2,1)} fusion(bf16[2,1024,1536]{2,1,0:T(8,128)(2,1)} %copy-done.3, bf16[2,1024,768]{2,1,0:T(8,128)(2,1)} %get-tuple-element.78), kind=kOutput, calls=%fused_computation.11 | convolution fusion | flops 4833017856 | bytes 11796480 | tf_op jit(solution)/shard_map/btd,btk->dk/dot_general | solution.py:1002
  238.9 26.8 %chain.3.carried_ref = f32[2,128,768]{2,1,0:T(8,128)} custom-call(f32[2,128,768]{2,1,0:T(8,128)} %get-tuple-element.77.own_ref, f32[2,8,768]{2,1,0:T(8,128)} %reshape.142.tot_ref), custom_call_target="tpu_custom_call" | custom-call | tf_op jit(solution)/shard_map/chain/pallas_call | solution.py:716
  265.7 7.4 %bitcast_convert_fusion = bf16[1536,768]{1,0:T(8,128)(2,1)S(1)} fusion(bf16[2,1024,1536]{2,1,0:T(8,128)(2,1)} %copy-done.1, bf16[2,1024,768]{2,1,0:T(8,128)(2,1)S(1)} %copy-done.8), kind=kOutput, calls=%fused_computation.10 | convolution fusion | flops 4833017856 | bytes 11796480 | tf_op jit(solution)/shard_map/btd,btk->dk/dot_general | solution.py:1003
  273.1 2.5 pad_maximum_fusion
  275.6 10.7 %reduce-scatter.5.cloned.1.call-start = ((), (), s32[]{:S(2)}) async-start(), calls=%async_computation.5 | async-start | bytes 3981312 | tf_op jit(solution)/shard_map/reduce_scatter | solution.py:1088
  286.3 42.8 %ssd_backward.1 = (bf16[2,1024,1920]{2,1,0:T(8,128)(2,1)}, f32[2,8,1152]{2,1,0:T(8,128)}, f32[8,768]{1,0:T(8,128)}, f32[8,256]{1,0:T(8,128)}, f32[8,128]{1,0:T(8,128)}) custom-call(f32[2,1024,768]{2,1,0:T(8,128)} %get-tuple-element.71.grad_ref, bf16[2,1024,768]{2,1,0:T(8,128)(2,1)} %get-tuple-element.72.cgate_ref, f32[2,1024,768]{2,1,0:T(8,128)} %get-tuple-element.61.x_ref, ...), custom_call_target="tpu_custom_call" | custom-call | tf_op jit(solution)/shard_map/ssd_backward/pallas_call | solution.py:1012
  331.3 7.0 %convolution_convert_fusion.in_ref = bf16[2,1024,1536]{2,1,0:T(8,128)(2,1)S(1)} fusion(bf16[2,1024,768]{2,1,0:T(8,128)(2,1)S(1)} %copy-done.26, bf16[1536,768]{1,0:T(8,128)(2,1)} %all-gather.5.cloned.1.call-done), kind=kOutput, calls=%fused_computation.6 | convolution fusion | flops 4834983936 | bytes 11796480 | tf_op jit(solution)/shard_map/btk,dk->btd/dot_general | solution.py:1009
  339.1 38.8 %scatter_tokens.2 = f32[2,256,1536]{2,1,0:T(8,128)S(1)} custom-call(bf16[2,1024,1536]{2,1,0:T(8,128)(2,1)S(1)} %convolution_convert_fusion.in_ref), custom_call_target="tpu_custom_call" | custom-call | tf_op jit(solution)/shard_map/scatter_tokens/pallas_call | solution.py:638
  377.8 1.7 copy-done
  380.9 13.1 %fusion = bf16[1536,1152]{1,0:T(8,128)(2,1)} fusion(bf16[2,1024,1536]{2,1,0:T(8,128)(2,1)} %copy-done.1, bf16[2,1024,1920]{2,1,0:T(8,128)(2,1)} %add_dynamic-update-slice_fusion), kind=kOutput, calls=%fused_computation.1 | convolution fusion | flops 7249526784 | bytes 14548992 | tf_op jit(solution)/shard_map/btd,btk->dk/dot_general | solution.py:1083
  395.2 17.5 %fusion.5.in_ref = bf16[2,1024,1536]{2,1,0:T(8,128)(2,1)S(1)} fusion(bf16[2,1024,1920]{2,1,0:T(8,128)(2,1)} %add_dynamic-update-slice_fusion, bf16[1536,1920]{1,0:T(8,128)(2,1)} %all-gather.3.cloned.1.call-done), kind=kOutput, calls=%fused_computation.7 | convolution fusion | flops 12082741248 | bytes 20054016 | tf_op jit(solution)/shard_map/btk,dk->btd/dot_general | solution.py:1089
  412.7 38.7 %scatter_tokens.3 = f32[2,256,1536]{2,1,0:T(8,128)S(1)} custom-call(bf16[2,1024,1536]{2,1,0:T(8,128)(2,1)S(1)} %fusion.5.in_ref), custom_call_target="tpu_custom_call" | custom-call | tf_op jit(solution)/shard_map/scatter_tokens/pallas_call | solution.py:638
  453.1 14.9 %small_sum.4 = f32[64,128]{1,0:T(8,128)} custom-call(f32[64,128]{1,0:T(8,128)} %pad_maximum_fusion.1.in_ref), custom_call_target="tpu_custom_call" | custom-call | tf_op jit(solution)/shard_map/small_sum/pallas_call | solution.py:775
  470.4 4.3 fusion.29
  474.7 2.8 copy.55
  478.1 2.8 copy.54
  486.7 12.6 %small_sum.5 = f32[384,128]{1,0:T(8,128)} custom-call(f32[384,128]{1,0:T(8,128)} %reshape.156.in_ref), custom_call_target="tpu_custom_call" | custom-call | tf_op jit(solution)/shard_map/small_sum/pallas_call | solution.py:775
  500.4 1.9 copy.56
  (127 shorter events, 29.9 us)
Async XLA Ops:
  7.2 102.2 %all-gather.3.cloned.1.call-start = ((), (), s32[]{:S(2)}) async-start(), calls=%async_computation.2 | async-start | bytes 6635520 | tf_op jit(solution)/shard_map/all_gather | solution.py:860
  9.0 3.7 copy-start.6
  11.5 1.7 copy-start.4
  11.6 2.0 copy-start.13
  12.6 156.4 %all-gather.5.cloned.1.call-start = ((), (), s32[]{:S(2)}) async-start(), calls=%async_computation.3 | async-start | bytes 2654208 | tf_op jit(solution)/shard_map/all_gather | solution.py:862
  13.6 74.2 %copy-start.15 = (f32[2,256]{1,0:T(2,128)}, f32[2,256]{1,0:T(2,128)S(1)}, u32[]{:S(2)}) copy-start(f32[2,256]{1,0:T(2,128)S(1)} %add_rsqrt_fusion) | copy-start | bytes 6148
  13.6 83.3 %copy-start.20 = (f32[768]{0:T(1024)S(1)}, f32[768]{0:T(1024)}, u32[]{:S(2)}) copy-start(f32[768]{0:T(1024)} %param.23) | copy-start | bytes 9220
  13.6 83.3 %copy-start.21 = (f32[768]{0:T(1024)S(1)}, f32[768]{0:T(1024)}, u32[]{:S(2)}) copy-start(f32[768]{0:T(1024)} %param.29) | copy-start | bytes 9220
  13.6 83.3 %copy-start.22 = (f32[4,2,128]{2,1,0:T(2,128)S(1)}, f32[4,2,128]{2,1,0:T(2,128)}, u32[]{:S(2)}) copy-start(f32[4,2,128]{2,1,0:T(2,128)} %param.24) | copy-start | bytes 12292
  13.7 83.3 %copy-start.24 = (f32[12]{0:T(128)S(1)}, f32[12]{0:T(128)}, u32[]{:S(2)}) copy-start(f32[12]{0:T(128)} %param.28) | copy-start | bytes 148
  13.7 83.4 %copy-start.27 = (f32[12]{0:T(128)S(1)}, f32[12]{0:T(128)}, u32[]{:S(2)}) copy-start(f32[12]{0:T(128)} %param.27) | copy-start | bytes 148
  13.7 83.4 %copy-start.23 = (f32[2,128]{1,0:T(2,128)S(1)}, f32[2,128]{1,0:T(2,128)}, u32[]{:S(2)}) copy-start(f32[2,128]{1,0:T(2,128)} %param.25) | copy-start | bytes 3076
  13.7 84.1 %copy-start.18 = (f32[4,768]{1,0:T(4,128)S(1)}, f32[4,768]{1,0:T(4,128)}, u32[]{:S(2)}) copy-start(f32[4,768]{1,0:T(4,128)} %param.22) | copy-start | bytes 36868
  13.7 85.5 %copy-start.25 = (f32[12]{0:T(128)S(1)}, f32[12]{0:T(128)}, u32[]{:S(2)}) copy-start(f32[12]{0:T(128)} %param.26) | copy-start | bytes 148
  87.8 2.7 copy-start.3
  90.5 2.7 copy-start.1
  93.2 16.3 %collective-permute-start = (bf16[2,8,1536]{2,1,0:T(8,128)(2,1)S(1)}, bf16[2,8,1536]{2,1,0:T(8,128)(2,1)S(1)}, u32[]{:S(2)}, u32[]{:S(2)}) collective-permute-start(bf16[2,8,1536]{2,1,0:T(8,128)(2,1)S(1)} %slice.132), channel_id=1, source_target_pairs={{0,4},{4,8},{8,12},{1,5},{5,9},{9,13},{2,6},{6,10},{10,14},{3,7},{... | collective-permute-start | bytes 147464 | tf_op jit(solution)/shard_map/ppermute | solution.py:794
  109.4 284.6 %reduce-scatter.3.cloned.1.call-start = ((), (), s32[]{:S(2)}) async-start(), calls=%async_computation.4 | async-start | bytes 5308416 | tf_op jit(solution)/shard_map/reduce_scatter | solution.py:1008
  109.4 3.9 copy-start.2
  229.5 36.1 %copy-start.8 = (bf16[2,1024,768]{2,1,0:T(8,128)(2,1)S(1)}, bf16[2,1024,768]{2,1,0:T(8,128)(2,1)}, u32[]{:S(2)}) copy-start(bf16[2,1024,768]{2,1,0:T(8,128)(2,1)} %get-tuple-element.72.cgate_ref) | copy-start | bytes 9437188
  265.6 7.4 %copy-start.9 = (bf16[1536,768]{1,0:T(8,128)(2,1)S(1)}, bf16[1536,768]{1,0:T(8,128)(2,1)}, u32[]{:S(2)}) copy-start(bf16[1536,768]{1,0:T(8,128)(2,1)} %bitcast_convert_fusion.1) | copy-start | bytes 7077892
  275.6 208.0 %reduce-scatter.5.cloned.1.call-start = ((), (), s32[]{:S(2)}) async-start(), calls=%async_computation.5 | async-start | bytes 3981312 | tf_op jit(solution)/shard_map/reduce_scatter | solution.py:1088
  286.3 45.0 %copy-start.26 = (bf16[2,1024,768]{2,1,0:T(8,128)(2,1)S(1)}, bf16[2,1024,768]{2,1,0:T(8,128)(2,1)}, u32[]{:S(2)}) copy-start(bf16[2,1024,768]{2,1,0:T(8,128)(2,1)} %get-tuple-element.78) | copy-start | bytes 9437188
  330.0 49.5 %collective-permute-start.1 = (bf16[2,8,1152]{2,1,0:T(8,128)(2,1)S(1)}, bf16[2,8,1152]{2,1,0:T(8,128)(2,1)S(1)}, u32[]{:S(2)}, u32[]{:S(2)}) collective-permute-start(bf16[2,8,1152]{2,1,0:T(8,128)(2,1)S(1)} %convert.2), channel_id=1, source_target_pairs={{4,0},{8,4},{12,8},{5,1},{9,5},{13,9},{6,2},{10,6},{14,10},{7,3},{... | collective-permute-start | bytes 110600 | tf_op jit(solution)/shard_map/ppermute | solution.py:794
  412.7 38.7 %copy-start.5 = (bf16[256,2,1536]{2,1,0:T(2,128)(2,1)S(1)}, bf16[256,2,1536]{2,1,0:T(2,128)(2,1)}, u32[]{:S(2)}) copy-start(bf16[256,2,1536]{2,1,0:T(2,128)(2,1)} %param.17) | copy-start | bytes 4718596
  412.7 38.7 %copy-start.14 = (f32[1536]{0:T(1024)S(1)}, f32[1536]{0:T(1024)}, u32[]{:S(2)}) copy-start(f32[1536]{0:T(1024)} %param.18) | copy-start | bytes 18436
  412.7 38.7 %copy-start.16 = (f32[2,256]{1,0:T(2,128)S(1)}, f32[2,256]{1,0:T(2,128)}, u32[]{:S(2)}) copy-start(f32[2,256]{1,0:T(2,128)} %copy-done.15) | copy-start | bytes 6148
  474.7 2.8 slice-start
  474.7 3.4 copy-start.7
  474.7 6.2 %copy-start.12 = (f32[64,128]{1,0:T(8,128)S(1)}, f32[64,128]{1,0:T(8,128)}, u32[]{:S(2)}) copy-start(f32[64,128]{1,0:T(8,128)} %small_sum.4) | copy-start | bytes 98308
  474.7 7.9 %copy-start.11 = (bf16[192,1536]{1,0:T(8,128)(2,1)S(1)}, bf16[192,1536]{1,0:T(8,128)(2,1)}, u32[]{:S(2)}) copy-start(bf16[192,1536]{1,0:T(8,128)(2,1)} %reduce-scatter.3.cloned.1.call-done) | copy-start | bytes 1769476
  499.3 3.0 copy-start.10
  (3 other events, 3.8 us)
Sparse Core Ops, SparseCore 0:
  12.7 96.6 all-gather.2
  111.4 54.4 all-gather.4
  275.7 92.8 reduce-scatter.2
  394.2 80.8 reduce-scatter.4

commit v3 on v2

--- a/solution.py
+++ b/solution.py
@@ -734,7 +734,7 @@
     bufs, sends, recvs = scratch[:count], scratch[count : 2 * count], scratch[2 * count :]
     barrier = pltpu.get_barrier_semaphore()
     greeted = 0
-    for axis, _ in phases:
+    for axis, _, _ in phases:
         me, size = lax.axis_index(axis), lax.axis_size(axis)
         for d in range(1, size):
             peer = lax.rem(me + d, size)
@@ -742,10 +742,10 @@
             greeted += 1
     pl.semaphore_wait(barrier, greeted)
     out_ref[...] = in_ref[...]
-    for p, (axis, first) in enumerate(phases):
+    for p, (axis, first, stop) in enumerate(phases):
         me, size = lax.axis_index(axis), lax.axis_size(axis)
-        rows = in_ref.shape[0] - first
-        bufs[p][pl.ds(me, 1)] = out_ref[first:, :].reshape(1, rows, LANES)
+        rows = stop - first
+        bufs[p][pl.ds(me, 1)] = out_ref[first:stop, :].reshape(1, rows, LANES)
         copies = []
         for d in range(1, size):
             copies.append(
@@ -764,13 +764,14 @@
         total = bufs[p][0]
         for r in range(1, size):
             total = total + bufs[p][r]
-        out_ref[first:, :] = total
+        out_ref[first:stop, :] = total
 
 
 def small_sum(value, phases, ident):
-    rows = value.shape[0]
-    sizes = [lax.axis_size(axis) for axis, _ in phases]
-    scratch = [pltpu.VMEM((n, rows - first, LANES), F32) for n, (_, first) in zip(sizes, phases)]
+    sizes = [lax.axis_size(axis) for axis, _, _ in phases]
+    scratch = [
+        pltpu.VMEM((n, stop - first, LANES), F32) for n, (_, first, stop) in zip(sizes, phases)
+    ]
     scratch += [pltpu.SemaphoreType.DMA((max(n - 1, 1),)) for n in sizes] * 2
     return pl.pallas_call(
         functools.partial(sum_kernel, phases),
@@ -963,7 +964,8 @@
         name="ssd_forward",
     )(x_act, bc_act, step, cum, pre, grad_hidden, state_in, chan)
 
-    stats = small_sum(stats.reshape(-1, LANES), (("tensor", 0),), 4).reshape(stats.shape)
+    rows = stats.size // LANES
+    stats = small_sum(stats.reshape(rows, LANES), (("tensor", 0, rows),), 4).reshape(stats.shape)
 
     grad_mixed, cot_gate, hidden, ds_local, sums_n = pl.pallas_call(
         functools.partial(gating_kernel, pairs, inner_total),
@@ -1004,10 +1006,12 @@
     grad_oz = with_layout_constraint(
         jnp.concatenate([grad_o, grad_z], axis=1), Layout(major_to_minor=(0, 1))
     )
-    carried, grad_oz = lax.optimization_barrier((carried, grad_oz))
+    carried, grad_oz, hidden = lax.optimization_barrier((carried, grad_oz, hidden))
     red_oz = lax.psum_scatter(grad_oz, pspace, scatter_dimension=0, tiled=True)
     branch_part = jnp.einsum("btk,dk->btd", hidden, full_o, preferred_element_type=F32).astype(BF)
     branch = scatter_tokens(branch_part, 1)
+    carried, branch = lax.optimization_barrier((carried, branch))
+    block_output = jnp.swapaxes((flat_in + branch).astype(BF), 0, 1)
 
     cot_in, tail, sums_x, sums_bc, sums_dt = pl.pallas_call(
         functools.partial(backward_kernel, pairs),
@@ -1081,10 +1085,7 @@
     cot_in = cot_in.at[:, span - 8 :, width:].add(later.astype(BF))
 
     grad_wx = jnp.einsum("btd,btk->dk", normed, cot_in[..., width:], preferred_element_type=F32)
-    grad_wx, cot_in, red_oz, branch = lax.optimization_barrier(
-        (grad_wx.astype(BF), cot_in, red_oz, branch)
-    )
-    block_output = jnp.swapaxes((flat_in + branch).astype(BF), 0, 1)
+    grad_wx, cot_in, red_oz = lax.optimization_barrier((grad_wx.astype(BF), cot_in, red_oz))
     red_x = lax.psum_scatter(grad_wx, pspace, scatter_dimension=0, tiled=True)
     part = jnp.einsum("btk,dk->btd", cot_in, full_in, preferred_element_type=F32).astype(BF)
     grad_normed = scatter_tokens(part, 2)
@@ -1103,13 +1104,17 @@
     )
     mine = rows_of_lanes(jnp.concatenate(sizes_own))
     rest = rows_of_lanes(jnp.concatenate([sums_bc[:5].reshape(-1), gain_part]))
+    part_bc = red_x[:, width : width + 2 * state_n].astype(F32).reshape(-1, LANES)
     first = mine.shape[0]
+    second = first + rest.shape[0]
+    third = second + part_bc.shape[0]
     summed = small_sum(
-        jnp.concatenate([mine, rest], 0), (("dp", 0), ("seq", 0), ("tensor", first)), 6
-    )
-    own, shared = summed[:first].reshape(-1), summed[first:].reshape(-1)
-    part_bc = red_x[:, width : width + 2 * state_n].astype(F32)
-    grad_bc = small_sum(part_bc.reshape(-1, LANES), (("tensor", 0),), 7)
+        jnp.concatenate([mine, rest, part_bc], 0),
+        (("dp", 0, second), ("seq", 0, second), ("tensor", first, third)),
+        6,
+    )
+    own, shared = summed[:first].reshape(-1), summed[first:second].reshape(-1)
+    grad_bc = summed[second:]
 
     n5 = 5 * inner
     bc5 = 5 * 2 * state_n

time: 515 us -> 514 us (level)
  waiting for transfers between devices: 9.62 us -> 24.5 us
  Pallas kernels: 332 us -> 321 us
  starting transfers between devices: 15.6 us -> 5.49 us
    reduce_scatter x1, waiting for transfers between devices: 0.01 us -> 10.4 us  [shards(): red_x = lax.psum_scatter(grad_wx, pspace, scatter_dimension=0, tiled=True)]
    reduce_scatter x1, starting transfers between devices: 10.7 us -> 0.45 us  [shards(): red_x = lax.psum_scatter(grad_wx, pspace, scatter_dimension=0, tiled=True)]
    pallas_call x3 -> x2, Pallas kernels: 32.6 us -> 23.9 us  [small_sum(): pl.pallas_call(functools.partial(sum_kernel, phases), out_shape=jax.Shape...]
    unnamed x65 -> x58, local copies, waits for them, and re-layouts: 18.7 us -> 18.1 us
  transfers between devices with their start and end apart: 6 -> 6, of which waited for: 1 -> 3; matrix products, arithmetic and copies ran while one was open for 17% -> 15% of each run, Pallas kernels for 48% -> 45%
where the time goes in v3:
time: 514 us; the launch traced here: 504 us
  Pallas kernels  321 us (62%)
  matrix products  85.8 us (17%)
  local copies, waits for them, and re-layouts  38.1 us (7%)
  waiting for transfers between devices  24.5 us (5%)
  between operations  14.5 us (3%)
  other arithmetic  14.4 us (3%)
  starting transfers between devices  5.49 us (1%)
    pallas_call x2, Pallas kernels, scatter_tokens(): pl.pallas_call(functools.partial(scatter_kernel, cuts), out_shape=jax.Sha...  75.5 us
    pallas_call x1, Pallas kernels, gather_tokens(): pl.pallas_call(functools.partial(gather_kernel, cuts, count), out_shape=[...  73.7 us
    pallas_call x2, Pallas kernels, chain(): pl.pallas_call(functools.partial(chain_kernel, by, cuts), out_shape=jax.S...  43.4 us
    pallas_call x1, Pallas kernels, shards(): pl.pallas_call(functools.partial(backward_kernel, pairs), grid=grid, out_...  42.7 us
    pallas_call x1, Pallas kernels, shards(): pl.pallas_call(functools.partial(forward_kernel, pairs), grid=grid, out_s...  24.5 us
    pallas_call x2, Pallas kernels, small_sum(): pl.pallas_call(functools.partial(sum_kernel, phases), out_shape=jax.Shape...  23.9 us
    pallas_call x1, Pallas kernels, shards(): pl.pallas_call(functools.partial(acts_kernel, pairs), grid=grid, out_shap...  18.9 us
    pallas_call x1, Pallas kernels, shards(): pl.pallas_call(functools.partial(gating_kernel, pairs, inner_total), grid...  18.5 us
  transfers between devices with their start and end apart: 6, of which 3 were waited for; matrix products, arithmetic and copies ran while one was open for 15% of the time, Pallas kernels for 45%

profile of v3, /device:TPU:0, one launch (start us, length us, event | category | flops | bytes accessed | tf_op | source)
XLA Modules:
  0.0 503.9 jit_solution(1157692100451893050)
XLA Ops:
  9.0 2.6 fusion.33
  14.2 73.7 %gather_tokens.1 = (bf16[2,1024,1536]{2,1,0:T(8,128)(2,1)S(1)}, bf16[2,1024,1536]{2,1,0:T(8,128)(2,1)S(1)}) custom-call(bf16[2,256,1536]{2,1,0:T(8,128)(2,1)S(1)} %fusion.16.refs_0_, bf16[2,256,1536]{2,1,0:T(8,128)(2,1)S(1)} %bitcast.117), custom_call_target="tpu_custom_call" | custom-call | tf_op jit(solution)/shard_map/gather_tokens/pallas_call | solution.py:558
  87.8 2.6 copy-done.2
  90.5 2.6 copy-done
  93.1 3.5 collective-permute-start
  99.7 9.6 %all-gather.3.cloned.1.call-done = bf16[1536,1920]{1,0:T(8,128)(2,1)} async-done(((bf16[192,1920]{1,0:T(8,128)(2,1)}), bf16[1536,1920]{1,0:T(8,128)(2,1)}) %all-gather.3.cloned.1.call-update) | async-done | bytes 5898256 | tf_op jit(solution)/shard_map/all_gather | solution.py:861
  109.4 3.4 fusion.9.halo_ref
  113.3 18.5 %fusion.3.x_ref.bc_ref.dt_ref.gate_ref.px_ref.pbc_ref.pdt_ref = f32[2,1024,1920]{2,1,0:T(8,128)} fusion(bf16[2,1024,1536]{2,1,0:T(8,128)(2,1)S(1)} %copy-done.1, bf16[1536,1920]{1,0:T(8,128)(2,1)} %all-gather.3.cloned.1.call-done), kind=kOutput, calls=%fused_computation.4 | convolution fusion | flops 12079595520 | bytes 27918336 | tf_op jit(solution)/shard_map/btd,dk->btk/dot_general | solution.py:887
  131.8 18.9 %acts.1 = (f32[2,1024,768]{2,1,0:T(8,128)}, bf16[2,1024,768]{2,1,0:T(8,128)(2,1)}, f32[2,1024,256]{2,1,0:T(8,128)}, bf16[2,1024,256]{2,1,0:T(8,128)(2,1)}, f32[2...) custom-call(f32[2,1024,1920]{2,1,0:T(8,128)} %fusion.3.x_ref.bc_ref.dt_ref.gate_ref, ...), custom_call_target="tpu_custom_call" | custom-call | tf_op jit(solution)/shard_map/acts/pallas_call | solution.py:897
  152.2 16.7 %chain.2.in_ref = f32[2,128,768]{2,1,0:T(8,128)} custom-call(f32[2,128,768]{2,1,0:T(8,128)} %get-tuple-element.69.own_ref, f32[2,8,768]{2,1,0:T(8,128)} %reshape.143.tot_ref), custom_call_target="tpu_custom_call" | custom-call | tf_op jit(solution)/shard_map/chain/pallas_call | solution.py:716
  168.9 9.5 %fusion.26.gh_ref = f32[2,1024,768]{2,1,0:T(8,128)} fusion(bf16[2,1024,1536]{2,1,0:T(8,128)(2,1)} %copy-done.2, bf16[1536,768]{1,0:T(8,128)(2,1)} %all-gather.5.cloned.1.call-done), kind=kOutput, calls=%fused_computation.32 | convolution fusion | flops 4831838208 | bytes 14942208 | tf_op jit(solution)/shard_map/btd,dk->btk/dot_general | solution.py:889
  178.4 24.5 %ssd_forward.1 = (f32[2,1024,768]{2,1,0:T(8,128)}, bf16[2,4,128,768]{3,2,1,0:T(8,128)(2,1)}, f32[2,4,128,768]{3,2,1,0:T(8,128)}, f32[2,2,1024]{2,1,0:T(2,128)}) custom-call(f32[2,1024,768]{2,1,0:T(8,128)} %get-tuple-element.63.x_ref, f32[2,1024,256]{2,1,0:T(8,128)} %get-tuple-element.64.bc_ref, f32[2,1024,128]{2,1,0:T(8,128)} %get-tuple-element.68.time_ref, ...), custom_call_target="tpu_custom_call" | custom-call | tf_op jit(solution)/shard_map/ssd_forward/pallas_call | solution.py:937
  204.3 5.1 %small_sum.2 = f32[32,128]{1,0:T(8,128)} custom-call(f32[32,128]{1,0:T(8,128)} %reshape.144.in_ref), custom_call_target="tpu_custom_call" | custom-call | tf_op jit(solution)/shard_map/small_sum/pallas_call | solution.py:776
  210.7 18.5 %gating_backward.1 = (f32[2,1024,768]{2,1,0:T(8,128)}, bf16[2,1024,768]{2,1,0:T(8,128)(2,1)}, bf16[2,1024,768]{2,1,0:T(8,128)(2,1)}, f32[2,128,768]{2,1,0:T(8,128)}, f32[8,768]{1,0:T(8,128)}) custom-call(f32[2,1024,768]{2,1,0:T(8,128)} %get-tuple-element.63.x_ref, f32[2,1024,256]{2,1,0:T(8,128)} %get-tuple-element.64.bc_ref, ...), custom_call_target="tpu_custom_call" | custom-call | tf_op jit(solution)/shard_map/gating_backward/pallas_call | solution.py:970
  229.3 9.4 %bitcast_convert_fusion.1 = bf16[1536,768]{1,0:T(8,128)(2,1)} fusion(bf16[2,1024,1536]{2,1,0:T(8,128)(2,1)} %copy-done.2, bf16[2,1024,768]{2,1,0:T(8,128)(2,1)} %get-tuple-element.77), kind=kOutput, calls=%fused_computation.11 | convolution fusion | flops 4833017856 | bytes 11796480 | tf_op jit(solution)/shard_map/btd,btk->dk/dot_general | solution.py:1004
  238.7 26.8 %chain.3.carried_ref = f32[2,128,768]{2,1,0:T(8,128)} custom-call(f32[2,128,768]{2,1,0:T(8,128)} %get-tuple-element.73.own_ref, f32[2,8,768]{2,1,0:T(8,128)} %reshape.143.tot_ref), custom_call_target="tpu_custom_call" | custom-call | tf_op jit(solution)/shard_map/chain/pallas_call | solution.py:716
  265.5 7.4 %bitcast_convert_fusion = bf16[1536,768]{1,0:T(8,128)(2,1)S(1)} fusion(bf16[2,1024,1536]{2,1,0:T(8,128)(2,1)} %copy-done, bf16[2,1024,768]{2,1,0:T(8,128)(2,1)S(1)} %copy-done.7), kind=kOutput, calls=%fused_computation.10 | convolution fusion | flops 4833017856 | bytes 11796480 | tf_op jit(solution)/shard_map/btd,btk->dk/dot_general | solution.py:1005
  272.9 2.5 pad_maximum_fusion
  277.3 7.0 %convolution_convert_fusion.in_ref = bf16[2,1024,1536]{2,1,0:T(8,128)(2,1)S(1)} fusion(bf16[2,1024,768]{2,1,0:T(8,128)(2,1)S(1)} %copy-done.23, bf16[1536,768]{1,0:T(8,128)(2,1)} %all-gather.5.cloned.1.call-done), kind=kOutput, calls=%fused_computation.6 | convolution fusion | flops 4834983936 | bytes 11796480 | tf_op jit(solution)/shard_map/btk,dk->btd/dot_general | solution.py:1011
  284.2 38.8 %scatter_tokens.2 = f32[2,256,1536]{2,1,0:T(8,128)S(1)} custom-call(bf16[2,1024,1536]{2,1,0:T(8,128)(2,1)S(1)} %convolution_convert_fusion.in_ref), custom_call_target="tpu_custom_call" | custom-call | tf_op jit(solution)/shard_map/scatter_tokens/pallas_call | solution.py:638
  323.0 42.7 %ssd_backward.1 = (bf16[2,1024,1920]{2,1,0:T(8,128)(2,1)}, f32[2,8,1152]{2,1,0:T(8,128)}, f32[8,768]{1,0:T(8,128)}, f32[8,256]{1,0:T(8,128)}, f32[8,128]{1,0:T(8,128)}) custom-call(f32[2,1024,768]{2,1,0:T(8,128)} %get-tuple-element.79.grad_ref, bf16[2,1024,768]{2,1,0:T(8,128)(2,1)} %get-tuple-element.75.cgate_ref, f32[2,1024,768]{2,1,0:T(8,128)} %get-tuple-element.63.x_ref, ...), custom_call_target="tpu_custom_call" | custom-call | tf_op jit(solution)/shard_map/ssd_backward/pallas_call | solution.py:1016
  366.6 1.5 collective-permute-start.1
  368.1 4.4 collective-permute-done.1
  373.9 13.1 %fusion = bf16[1536,1152]{1,0:T(8,128)(2,1)} fusion(bf16[2,1024,1536]{2,1,0:T(8,128)(2,1)} %copy-done, bf16[2,1024,1920]{2,1,0:T(8,128)(2,1)} %add_dynamic-update-slice_fusion), kind=kOutput, calls=%fused_computation.1 | convolution fusion | flops 7249526784 | bytes 14548992 | tf_op jit(solution)/shard_map/btd,btk->dk/dot_general | solution.py:1087
  388.9 17.6 %fusion.5.in_ref = bf16[2,1024,1536]{2,1,0:T(8,128)(2,1)S(1)} fusion(bf16[2,1024,1920]{2,1,0:T(8,128)(2,1)} %add_dynamic-update-slice_fusion, bf16[1536,1920]{1,0:T(8,128)(2,1)} %all-gather.3.cloned.1.call-done), kind=kOutput, calls=%fused_computation.7 | convolution fusion | flops 12082741248 | bytes 20054016 | tf_op jit(solution)/shard_map/btk,dk->btd/dot_general | solution.py:1090
  406.5 36.7 %scatter_tokens.3 = f32[2,256,1536]{2,1,0:T(8,128)S(1)} custom-call(bf16[2,1024,1536]{2,1,0:T(8,128)(2,1)S(1)} %fusion.5.in_ref), custom_call_target="tpu_custom_call" | custom-call | tf_op jit(solution)/shard_map/scatter_tokens/pallas_call | solution.py:638
  446.1 2.8 copy.55
  448.8 2.8 copy.54
  452.5 10.4 %reduce-scatter.5.cloned.1.call-done = bf16[192,1152]{1,0:T(8,128)(2,1)} async-done(((bf16[1536,1152]{1,0:T(8,128)(2,1)}), bf16[192,1152]{1,0:T(8,128)(2,1)}) %reduce-scatter.5.cloned.1.call-update) | async-done | bytes 442384 | tf_op jit(solution)/shard_map/reduce_scatter | solution.py:1089
  464.5 18.8 %small_sum.3 = f32[448,128]{1,0:T(8,128)} custom-call(f32[448,128]{1,0:T(8,128)} %pad_maximum_fusion.1.in_ref), custom_call_target="tpu_custom_call" | custom-call | tf_op jit(solution)/shard_map/small_sum/pallas_call | solution.py:776
  489.8 1.6 slice.151
  495.2 1.9 copy.56
  (119 shorter events, 33.8 us)
Async XLA Ops:
  7.2 102.2 %all-gather.3.cloned.1.call-start = ((), (), s32[]{:S(2)}) async-start(), calls=%async_computation.2 | async-start | bytes 6635520 | tf_op jit(solution)/shard_map/all_gather | solution.py:861
  9.0 3.7 copy-start.5
  11.5 1.7 copy-start.3
  11.6 2.0 copy-start.10
  12.6 156.3 %all-gather.5.cloned.1.call-start = ((), (), s32[]{:S(2)}) async-start(), calls=%async_computation.3 | async-start | bytes 2654208 | tf_op jit(solution)/shard_map/all_gather | solution.py:863
  13.6 74.2 %copy-start.12 = (f32[2,256]{1,0:T(2,128)}, f32[2,256]{1,0:T(2,128)S(1)}, u32[]{:S(2)}) copy-start(f32[2,256]{1,0:T(2,128)S(1)} %add_rsqrt_fusion) | copy-start | bytes 6148
  13.6 83.2 %copy-start.17 = (f32[768]{0:T(1024)S(1)}, f32[768]{0:T(1024)}, u32[]{:S(2)}) copy-start(f32[768]{0:T(1024)} %param.23) | copy-start | bytes 9220
  13.6 83.2 %copy-start.18 = (f32[768]{0:T(1024)S(1)}, f32[768]{0:T(1024)}, u32[]{:S(2)}) copy-start(f32[768]{0:T(1024)} %param.29) | copy-start | bytes 9220
  13.6 83.2 %copy-start.19 = (f32[4,2,128]{2,1,0:T(2,128)S(1)}, f32[4,2,128]{2,1,0:T(2,128)}, u32[]{:S(2)}) copy-start(f32[4,2,128]{2,1,0:T(2,128)} %param.24) | copy-start | bytes 12292
  13.7 83.2 %copy-start.21 = (f32[12]{0:T(128)S(1)}, f32[12]{0:T(128)}, u32[]{:S(2)}) copy-start(f32[12]{0:T(128)} %param.28) | copy-start | bytes 148
  13.7 83.4 %copy-start.24 = (f32[12]{0:T(128)S(1)}, f32[12]{0:T(128)}, u32[]{:S(2)}) copy-start(f32[12]{0:T(128)} %param.27) | copy-start | bytes 148
  13.7 83.4 %copy-start.20 = (f32[2,128]{1,0:T(2,128)S(1)}, f32[2,128]{1,0:T(2,128)}, u32[]{:S(2)}) copy-start(f32[2,128]{1,0:T(2,128)} %param.25) | copy-start | bytes 3076
  13.7 84.0 %copy-start.15 = (f32[4,768]{1,0:T(4,128)S(1)}, f32[4,768]{1,0:T(4,128)}, u32[]{:S(2)}) copy-start(f32[4,768]{1,0:T(4,128)} %param.22) | copy-start | bytes 36868
  13.7 85.4 %copy-start.22 = (f32[12]{0:T(128)S(1)}, f32[12]{0:T(128)}, u32[]{:S(2)}) copy-start(f32[12]{0:T(128)} %param.26) | copy-start | bytes 148
  87.8 2.6 copy-start.2
  90.5 2.6 copy-start
  93.1 16.3 %collective-permute-start = (bf16[2,8,1536]{2,1,0:T(8,128)(2,1)S(1)}, bf16[2,8,1536]{2,1,0:T(8,128)(2,1)S(1)}, u32[]{:S(2)}, u32[]{:S(2)}) collective-permute-start(bf16[2,8,1536]{2,1,0:T(8,128)(2,1)S(1)} %slice.135), channel_id=1, source_target_pairs={{0,4},{4,8},{8,12},{1,5},{5,9},{9,13},{2,6},{6,10},{10,14},{3,7},{... | collective-permute-start | bytes 147464 | tf_op jit(solution)/shard_map/ppermute | solution.py:795
  109.4 277.6 %reduce-scatter.3.cloned.1.call-start = ((), (), s32[]{:S(2)}) async-start(), calls=%async_computation.4 | async-start | bytes 5308416 | tf_op jit(solution)/shard_map/reduce_scatter | solution.py:1010
  109.4 3.9 copy-start.1
  229.3 36.2 %copy-start.7 = (bf16[2,1024,768]{2,1,0:T(8,128)(2,1)S(1)}, bf16[2,1024,768]{2,1,0:T(8,128)(2,1)}, u32[]{:S(2)}) copy-start(bf16[2,1024,768]{2,1,0:T(8,128)(2,1)} %get-tuple-element.75.cgate_ref) | copy-start | bytes 9437188
  265.4 7.4 %copy-start.8 = (bf16[1536,768]{1,0:T(8,128)(2,1)S(1)}, bf16[1536,768]{1,0:T(8,128)(2,1)}, u32[]{:S(2)}) copy-start(bf16[1536,768]{1,0:T(8,128)(2,1)} %bitcast_convert_fusion.1) | copy-start | bytes 7077892
  275.4 1.9 copy-start.23
  275.4 187.4 %reduce-scatter.5.cloned.1.call-start = ((), (), s32[]{:S(2)}) async-start(), calls=%async_computation.5 | async-start | bytes 3981312 | tf_op jit(solution)/shard_map/reduce_scatter | solution.py:1089
  366.6 5.8 %collective-permute-start.1 = (bf16[2,8,1152]{2,1,0:T(8,128)(2,1)S(1)}, bf16[2,8,1152]{2,1,0:T(8,128)(2,1)S(1)}, u32[]{:S(2)}, u32[]{:S(2)}) collective-permute-start(bf16[2,8,1152]{2,1,0:T(8,128)(2,1)S(1)} %convert.2), channel_id=1, source_target_pairs={{4,0},{8,4},{12,8},{5,1},{9,5},{13,9},{6,2},{10,6},{14,10},{7,3},{... | collective-permute-start | bytes 110600 | tf_op jit(solution)/shard_map/ppermute | solution.py:795
  387.0 1.1 copy-start.16
  387.0 1.1 copy-start.14
  406.5 36.8 %copy-start.4 = (bf16[256,2,1536]{2,1,0:T(2,128)(2,1)S(1)}, bf16[256,2,1536]{2,1,0:T(2,128)(2,1)}, u32[]{:S(2)}) copy-start(bf16[256,2,1536]{2,1,0:T(2,128)(2,1)} %param.17) | copy-start | bytes 4718596
  406.5 36.8 %copy-start.11 = (f32[1536]{0:T(1024)S(1)}, f32[1536]{0:T(1024)}, u32[]{:S(2)}) copy-start(f32[1536]{0:T(1024)} %param.18) | copy-start | bytes 18436
  406.5 36.8 %copy-start.13 = (f32[2,256]{1,0:T(2,128)S(1)}, f32[2,256]{1,0:T(2,128)}, u32[]{:S(2)}) copy-start(f32[2,256]{1,0:T(2,128)} %copy-done.12) | copy-start | bytes 6148
  443.3 1.4 copy-start.6
  446.0 5.5 %copy-start.9 = (bf16[192,1536]{1,0:T(8,128)(2,1)S(1)}, bf16[192,1536]{1,0:T(8,128)(2,1)}, u32[]{:S(2)}) copy-start(bf16[192,1536]{1,0:T(8,128)(2,1)} %reduce-scatter.3.cloned.1.call-done) | copy-start | bytes 1769476
Sparse Core Ops, SparseCore 0:
  12.7 96.6 all-gather.2
  111.4 54.3 all-gather.4
  275.5 92.8 reduce-scatter.2
  387.1 75.6 reduce-scatter.4
